TPU v7x, 16 devices: a 4x2x1 block of a 4x4x8 slice. The times are simulated.
16 devices in a mesh: dp: 2 (over y, z), tp: 8 (over x, core).
Axes of the slice: x: 4, y: 2, z: 1, core: 2. Of those that a mesh axis runs over, the one named last changes fastest.
The devices are a block of a 4x4x8 slice.
Arguments:
- x: bfloat16 [5632, 3072], P(('dp', 'tp')), parts along dimension 0
- dy: bfloat16 [5632, 3072], P(('dp', 'tp')), parts along dimension 0
- pre: bfloat16 [5632, 9216], P('dp', 'tp'), parts along dimension 0
- w_in: bfloat16 [3072, 9216], P(None, 'tp')
- w_down: bfloat16 [9216, 3072], P('tp')
Outputs:
- output 1: bfloat16 [5632, 3072], P(('dp', 'tp')), parts along dimension 0
- output 2: bfloat16 [6144, 9216], P('dp', 'tp'), parts along dimension 0
- output 3: bfloat16 [18432, 3072], P(('dp', 'tp')), parts along dimension 0
There are 2 independent parts. A program takes and returns all parts, laid end to end along the dimension named above; an argument that names none is the same for every part.
All inputs are finite; a program needn't handle non-finite values.
Results may differ from a plain program's by a relative error of at most 0.012.
Values are sent between devices in bfloat16 or wider.
A program may use at most 768 MiB of HBM per device.

v0:
```python
import jax
import jax.numpy as jnp


def act(pre):
    return jnp.square(jax.nn.relu(pre))


def solution(mesh):
    def step(x, dy, pre, w_in, w_down):
        hidden, back = jax.vjp(act, pre.astype(jnp.float32))
        d_hidden = jnp.dot(dy, w_down.T, preferred_element_type=jnp.float32)
        d_pre = back(d_hidden)[0].astype(jnp.bfloat16)
        dx = jnp.dot(d_pre, w_in.T)
        groups = mesh.shape["dp"]

        def by_group(a, b):
            a, b = (t.reshape(groups, -1, t.shape[-1]) for t in (a, b))
            product = jnp.einsum("gta,gtb->gab", a, b, preferred_element_type=jnp.float32)
            return product.astype(jnp.bfloat16).reshape(-1, b.shape[-1])

        return dx, by_group(x, d_pre), by_group(hidden.astype(jnp.bfloat16), dy)

    return step
```

profile of v0, /device:TPU:112, one launch (start us, length us, event | category | flops | bytes accessed | tf_op | source)
XLA Modules:
  0.0 281.5 jit_solution(10973344442740245225)
XLA Ops:
  7.2 0.1 all-gather.10.cloned.1.call-start
  7.2 0.7 all-gather.10.cloned.1.call-update
  8.0 0.1 all-gather.12.cloned.1.call-start
  8.0 0.7 all-gather.12.cloned.1.call-update
  8.8 0.1 reduce-scatter.4.cloned.1.call-start
  8.8 86.9 %all-gather.10.cloned.1.call-done = bf16[2816,3072]{1,0:T(8,128)(2,1)} async-done(((bf16[352,3072]{1,0:T(8,128)(2,1)}), bf16[2816,3072]{1,0:T(8,128)(2,1)}) %all-gather.10.cloned.1.call-update) | async-done | bytes 17301520 | tf_op args[1]
  95.8 28.6 %fusion.4 = bf16[2816,1152]{1,0:T(8,128)(2,1)S(1)} fusion(bf16[2816,1152]{1,0:T(8,128)(2,1)} %param, bf16[2816,3072]{1,0:T(8,128)(2,1)} %all-gather.10.cloned.1.call-done, bf16[1152,3072]{1,0:T(8,128)(2,1)} %param.2), kind=kOutput, calls=%fused_computation.9 | convolution fusion | flops 19954040832 | bytes 37355520 | tf_op jit(solution)/dot_general | solution.py:12
  124.4 0.0 copy-start
  124.4 2.8 copy-done
  127.2 27.8 %fusion.9 = bf16[2816,3072]{1,0:T(8,128)(2,1)} fusion(bf16[2816,1152]{1,0:T(8,128)(2,1)S(1)} %fusion.4, bf16[3072,1152]{1,0:T(8,128)(2,1)} %param.3), kind=kOutput, calls=%fused_computation.13 | convolution fusion | flops 19931332608 | bytes 30867456 | tf_op jit(solution)/dot_general | solution.py:14
  155.0 0.1 reduce-scatter.4.cloned.1.call-update
  155.1 26.2 %all-gather.12.cloned.1.call-done = bf16[2816,3072]{1,0:T(8,128)(2,1)} async-done(((bf16[352,3072]{1,0:T(8,128)(2,1)}), bf16[2816,3072]{1,0:T(8,128)(2,1)}) %all-gather.12.cloned.1.call-update) | async-done | bytes 17301520 | tf_op jit(solution)/reshape | solution.py:18
  181.3 26.5 %fusion.5 = bf16[3072,1152]{0,1:T(8,128)(2,1)} fusion(bf16[2816,1152]{1,0:T(8,128)(2,1)} %copy-done, bf16[2816,3072]{1,0:T(8,128)(2,1)} %all-gather.12.cloned.1.call-done), kind=kOutput, calls=%fused_computation.10 | convolution fusion | flops 19934871552 | bytes 30867456 | tf_op jit(solution)/gta,gtb->gab/dot_general | solution.py:19
  207.8 10.3 %copy = bf16[3072,1152]{1,0:T(8,128)(2,1)} copy(bf16[3072,1152]{0,1:T(8,128)(2,1)} %fusion.5) | data formatting | bytes 14155776
  218.1 26.8 %convolution_convert_fusion = bf16[1152,3072]{1,0:T(8,128)(2,1)} fusion(bf16[2816,3072]{1,0:T(8,128)(2,1)} %all-gather.10.cloned.1.call-done, bf16[2816,1152]{1,0:T(8,128)(2,1)} %param), kind=kOutput, calls=%fused_computation.7 | convolution fusion | flops 19947847680 | bytes 30867456 | tf_op jit(solution)/gta,gtb->gab/dot_general | solution.py:19
  244.8 30.2 %reduce-scatter.4.cloned.1.call-done = bf16[352,3072]{1,0:T(8,128)(2,1)} async-done(((bf16[2816,3072]{1,0:T(8,128)(2,1)}), bf16[352,3072]{1,0:T(8,128)(2,1)}) %reduce-scatter.4.cloned.1.call-update) | async-done | bytes 2162704
Async XLA Ops:
  7.2 88.6 %all-gather.10.cloned.1.call-start = ((), (), s32[]{:S(2)}) async-start(), calls=%async_computation.1 | async-start | bytes 19464192 | tf_op args[1]
  8.0 173.3 %all-gather.12.cloned.1.call-start = ((), (), s32[]{:S(2)}) async-start(), calls=%async_computation.2 | async-start | bytes 19464192 | tf_op jit(solution)/reshape | solution.py:18
  8.8 266.2 %reduce-scatter.4.cloned.1.call-start = ((), (), s32[]{:S(2)}) async-start(), calls=%async_computation.3 | async-start | bytes 19464192
  124.4 2.8 copy-start
Sparse Core Ops, SparseCore 0:
  9.6 86.1 all-gather.9
  97.4 83.8 all-gather.11
  184.2 90.7 reduce-scatter.3
where the time goes:
time: 282 us
  waiting for transfers between devices  145 us (51%)
  matrix products  110 us (39%)
  between operations  13.8 us (5%)
  local copies, waits for them, and re-layouts  13 us (5%)
    unnamed x5, waiting for transfers between devices  119 us
    dot_general x2, matrix products, by_group(): jnp.einsum('gta,gtb->gab', a, b, preferred_element_type=jnp.float32)  53.3 us
    dot_general x1, matrix products, step(): d_hidden = jnp.dot(dy, w_down.T, preferred_element_type=jnp.float32)  28.6 us
    dot_general x1, matrix products, step(): dx = jnp.dot(d_pre, w_in.T)  27.8 us
    reshape x1, waiting for transfers between devices, by_group(): a, b = (t.reshape(groups, -1, t.shape[-1]) for t in (a, b))  26.2 us
    unnamed x3, local copies, waits for them, and re-layouts  13 us
  transfers between devices with their start and end apart: 3, of which 3 were waited for; matrix products, arithmetic and copies ran while one was open for 43% of the time, Pallas kernels for 0%

commit v1 on v0

v1 whole, which is shorter than its diff:
```python
import functools

import jax
import jax.numpy as jnp
from jax import lax
from jax.experimental import pallas as pl
from jax.experimental.pallas import tpu as pltpu
from jax.sharding import PartitionSpec as P

CORES = 2
F32, BF16 = jnp.float32, jnp.bfloat16
NT = (((1,), (1,)), ((), ()))
TN = (((0,), (0,)), ((), ()))

(R0, R1, L0, L1, OWN, FR, FL, PL0, PL1, PR0, PR1, PO0, PO1) = range(13)
COPIES = 13


def gather_kernel(
    chips, x, dy, pre, w_in, w_down,
    xg, dyg, d_pre, s_own, s_left0, s_left1, s_right0, s_right1, s_far,
    wd_v, wi_v, wp_v, dy_v, pre_v, mine_v, other_v, got_v, acc_v, low_v,
    send_sem, recv_sem, got_send, got_recv, w_send, w_recv, load_sem, store_sem,
):
    rows, depth = dy.shape
    half = rows // 2
    cols = w_down.shape[0]
    me = lax.axis_index("tp")
    chip, core = me // CORES, lax.rem(me, CORES)
    left = lax.rem(chip + chips - 1, chips)
    right = lax.rem(chip + 1, chips)
    far = lax.rem(chip + 2, chips)

    def device(c, k):
        return {"tp": c * CORES + k}

    to_right, to_left, to_partner = device(right, core), device(left, core), device(chip, 1 - core)

    def block(ref, c, k, h=None):
        start = (c * CORES + k) * rows
        if h is None:
            return ref.at[pl.ds(pl.multiple_of(start, 16), rows)]
        return ref.at[pl.ds(pl.multiple_of(start + h * half, 16), half)]

    class Gather:
        def __init__(self, which, src, dst):
            self.which, self.src, self.dst = which, src, dst

        def own(self, h):
            return self.src.at[pl.ds(h * half, half)]

        def copy(self, n, src, dst, target):
            return pltpu.make_async_remote_copy(
                src_ref=src, dst_ref=dst, send_sem=send_sem.at[self.which, n], recv_sem=recv_sem.at[self.which, n],
                device_id=target, device_id_type=pl.DeviceIdType.MESH,
            )

        def out(self, n):
            d = self.dst
            if n in (R0, R1):
                h = n - R0
                return self.copy(n, self.own(h), block(d, chip, core, h), to_right)
            if n in (L0, L1):
                h = n - L0
                return self.copy(n, self.own(h), block(d, chip, core, h), to_left)
            if n == OWN:
                return self.copy(n, self.src, block(d, chip, core), to_partner)
            if n == FR:
                return self.copy(n, block(d, left, core, 0), block(d, left, core, 0), to_right)
            if n == FL:
                return self.copy(n, block(d, right, core, 1), block(d, right, core, 1), to_left)
            c, h = {PL0: (left, 0), PL1: (left, 1), PR0: (right, 0), PR1: (right, 1), PO0: (far, 0), PO1: (far, 1)}[n]
            return self.copy(n, block(d, c, core, h), block(d, c, core, h), to_partner)

        def start(self, *names):
            for n in names:
                self.out(n).start()

        def arrived(self, *names):
            for n in names:
                if n == OWN:
                    dst = block(self.dst, chip, 1 - core)
                else:
                    c, k, h = {
                        R0: (left, core, 0), R1: (left, core, 1), L0: (right, core, 0), L1: (right, core, 1),
                        FR: (far, core, 0), FL: (far, core, 1),
                        PL0: (left, 1 - core, 0), PL1: (left, 1 - core, 1), PR0: (right, 1 - core, 0),
                        PR1: (right, 1 - core, 1), PO0: (far, 1 - core, 0), PO1: (far, 1 - core, 1),
                    }[n]
                    dst = block(self.dst, c, k, h)
                self.copy(n, dst, dst, to_partner).wait_recv()

        def sent(self):
            for n in range(COPIES):
                self.out(n).wait_send()

    gy, gx = Gather(0, dy, dyg), Gather(1, x, xg)

    barrier = pltpu.get_barrier_semaphore()
    for target in (to_right, to_left, to_partner):
        pl.semaphore_signal(barrier, inc=1, device_id=target, device_id_type=pl.DeviceIdType.MESH)
    load_wd = pltpu.make_async_copy(w_down, wd_v, load_sem.at[0])
    load_dy = pltpu.make_async_copy(dy, dy_v, load_sem.at[1])
    load_x = pltpu.make_async_copy(x, low_v, load_sem.at[2])
    load_wi = pltpu.make_async_copy(w_in, wi_v, load_sem.at[3])
    load_dy.start()
    load_wd.start()
    pl.semaphore_wait(barrier, 3)

    gy.start(R0, L1, OWN, R1, L0)
    load_x.start()
    load_wi.start()
    give_w = pltpu.make_async_remote_copy(
        src_ref=w_in, dst_ref=wp_v, send_sem=w_send, recv_sem=w_recv,
        device_id=to_partner, device_id_type=pl.DeviceIdType.MESH,
    )
    give_w.start()

    load_dy.wait()
    keep_dy = pltpu.make_async_copy(dy_v, block(dyg, chip, core), store_sem.at[0])
    keep_dy.start()
    load_x.wait()
    keep_x = pltpu.make_async_copy(low_v, block(xg, chip, core), store_sem.at[1])
    keep_x.start()
    load_wd.wait()
    load_wi.wait()

    def chip_of(stage):
        return lax.rem(chip + jnp.where(stage == 0, 0, jnp.where(stage == 1, chips - 1, stage - 1)), chips)

    def hidden_grad(stage, k, out_v):
        c = chip_of(stage)
        load_pre = pltpu.make_async_copy(block(pre, c, k), pre_v, load_sem.at[0])
        load_pre.start()
        load = pltpu.make_async_copy(block(dyg, c, k), dy_v, load_sem.at[1])
        load.start()
        load.wait()
        load_pre.wait()
        tile = 384

        @pl.loop(0, cols // tile)
        def _(t):
            span = pl.ds(pl.multiple_of(t * tile, tile), tile)
            grad = lax.dot_general(dy_v[...], wd_v[span, :], NT, preferred_element_type=F32)
            p = pre_v[:, span].astype(F32)
            out_v[:, span] = jnp.where(p > 0, grad * (2.0 * p), 0.0).astype(BF16)

        keep = pltpu.make_async_copy(out_v, block(d_pre, c, k), store_sem.at[2])
        keep.start()
        return keep

    def swap(stage):
        return pltpu.make_async_remote_copy(
            src_ref=other_v, dst_ref=got_v.at[stage], send_sem=got_send, recv_sem=got_recv.at[stage],
            device_id=to_partner, device_id_type=pl.DeviceIdType.MESH,
        )

    keep_dy.wait()
    keep_x.wait()

    @pl.loop(0, chips)
    def _(stage):
        @pl.when(stage == 1)
        def _():
            gy.arrived(R0, L1)
            gy.start(FR, FL, PL0, PR1)
            gx.start(R0, L1, R1, L0, OWN)
            gy.arrived(R1, L0)
            gy.start(PL1, PR0)

        @pl.when(stage == 3)
        def _():
            gy.arrived(FR, FL)
            gy.start(PO0, PO1)

        hidden_grad(stage, core, mine_v).wait()

        @pl.when(stage == 0)
        def _():
            gy.arrived(OWN)

        @pl.when(stage == 1)
        def _():
            gy.arrived(PL0, PL1)

        @pl.when(stage == 2)
        def _():
            gy.arrived(PR0, PR1)

        @pl.when(stage == 3)
        def _():
            gy.arrived(PO0, PO1)

        keep = hidden_grad(stage, 1 - core, other_v)
        give = swap(stage)
        give.start()

        @pl.when(stage == 0)
        def _():
            give_w.wait()

        give.wait_recv()
        wide = 512

        @pl.loop(0, depth // wide)
        def _(t):
            span = pl.ds(pl.multiple_of(t * wide, wide), wide)
            term = lax.dot_general(mine_v[...], wi_v[span, :], NT, preferred_element_type=F32)
            term += lax.dot_general(got_v[stage], wp_v[span, :], NT, preferred_element_type=F32)
            acc_v[:, span] = term
            low_v[:, span] = term.astype(BF16)

        give.wait_send()
        keep.wait()
        top, bottom = pl.ds(0, half), pl.ds(half, half)

        def put(*pairs):
            copies = [pltpu.make_async_copy(s, d, store_sem.at[3 + i]) for i, (s, d) in enumerate(pairs)]
            for copy in copies:
                copy.start()
            for copy in copies:
                copy.wait()

        @pl.when(stage == 0)
        def _():
            put((acc_v, s_own))

        @pl.when(stage == 1)
        def _():
            put((low_v.at[top], s_left0), (acc_v.at[bottom], s_left1))

        @pl.when(stage == 2)
        def _():
            put((acc_v.at[top], s_right0), (low_v.at[bottom], s_right1))

        @pl.when(stage == 3)
        def _():
            put((low_v, s_far))

    gx.arrived(R0, L1)
    gx.start(FR, FL, PL0, PR1)
    gx.arrived(R1, L0)
    gx.start(PL1, PR0)
    gx.arrived(FR, FL)
    gx.start(PO0, PO1)
    gx.arrived(OWN, PL0, PL1, PR0, PR1, PO0, PO1)
    gy.sent()
    gx.sent()


def solution(mesh):
    n = mesh.shape["tp"]
    chips = n // CORES

    def gather(x, dy, pre, w_in, w_down):
        rows, depth = x.shape
        tokens, cols = pre.shape
        half = rows // 2
        anywhere = pl.BlockSpec(memory_space=pl.ANY)
        shape = jax.ShapeDtypeStruct
        return pl.pallas_call(
            functools.partial(gather_kernel, chips),
            name="gather",
            out_shape=(
                shape((tokens, depth), BF16),
                shape((tokens, depth), BF16),
                shape((tokens, cols), BF16),
                shape((rows, depth), F32),
                shape((half, depth), BF16),
                shape((half, depth), F32),
                shape((half, depth), F32),
                shape((half, depth), BF16),
                shape((rows, depth), BF16),
            ),
            in_specs=[anywhere] * 5,
            out_specs=(anywhere,) * 9,
            scratch_shapes=[
                pltpu.VMEM((cols, depth), BF16),
                pltpu.VMEM((depth, cols), BF16),
                pltpu.VMEM((depth, cols), BF16),
                pltpu.VMEM((rows, depth), BF16),
                pltpu.VMEM((rows, cols), BF16),
                pltpu.VMEM((rows, cols), BF16),
                pltpu.VMEM((rows, cols), BF16),
                pltpu.VMEM((chips, rows, cols), BF16),
                pltpu.VMEM((rows, depth), F32),
                pltpu.VMEM((rows, depth), BF16),
                pltpu.SemaphoreType.DMA((2, COPIES)),
                pltpu.SemaphoreType.DMA((2, COPIES)),
                pltpu.SemaphoreType.DMA,
                pltpu.SemaphoreType.DMA((chips,)),
                pltpu.SemaphoreType.DMA,
                pltpu.SemaphoreType.DMA,
                pltpu.SemaphoreType.DMA((4,)),
                pltpu.SemaphoreType.DMA((5,)),
            ],
            compiler_params=pltpu.CompilerParams(
                collective_id=0, has_side_effects=True, vmem_limit_bytes=64 * 1024 * 1024 - 65536
            ),
            cost_estimate=pl.CostEstimate(
                flops=4 * tokens * depth * cols, bytes_accessed=8 * tokens * depth, transcendentals=0
            ),
        )(x, dy, pre, w_in, w_down)

    def step(x, dy, pre, w_in, w_down):
        rows = x.shape[0]
        half = rows // 2
        clockwise = [(i, (i + CORES) % n) for i in range(n)]
        counter = [(i, (i - CORES) % n) for i in range(n)]
        xg, dyg, d_pre, s_own, s_left0, s_left1, s_right0, s_right1, s_far = gather(x, dy, pre, w_in, w_down)

        far0 = lax.ppermute(s_far[:half], "tp", clockwise)
        far1 = lax.ppermute(s_far[half:], "tp", counter)
        last1 = lax.ppermute(s_right1, "tp", clockwise)
        last0 = lax.ppermute(s_left0, "tp", counter)

        dw_in = lax.dot_general(xg, d_pre, TN, preferred_element_type=F32).astype(BF16)

        sum0 = lax.ppermute((s_right0 + far0.astype(F32)).astype(BF16), "tp", clockwise)
        sum1 = lax.ppermute((s_left1 + far1.astype(F32)).astype(BF16), "tp", counter)

        hidden = jnp.square(jax.nn.relu(pre.astype(F32))).astype(BF16)
        dw_down = lax.dot_general(hidden, dyg, TN, preferred_element_type=F32).astype(BF16)

        top = s_own[:half] + sum0.astype(F32) + last0.astype(F32)
        bottom = s_own[half:] + last1.astype(F32) + sum1.astype(F32)
        return jnp.concatenate([top, bottom]).astype(BF16), dw_in, dw_down

    tokens, columns, weight_rows = P(("dp", "tp"), None), P(None, "tp"), P("tp", None)
    return jax.shard_map(
        step,
        mesh=mesh,
        in_specs=(tokens, tokens, P("dp", "tp"), columns, weight_rows),
        out_specs=(tokens, P("dp", "tp"), P(("dp", "tp"), None)),
        check_vma=False,
    )
```

time: 282 us -> 234 us (0.83)
  Pallas kernels: 0 us -> 151 us
  waiting for transfers between devices: 145 us -> 14.8 us
  matrix products: 110 us -> 54.1 us
  between operations: 13.8 us -> 0.75 us
  local copies, waits for them, and re-layouts: 13 us -> 3.12 us
  starting transfers between devices: 0.18 us -> 7.54 us
  other arithmetic: 0 us -> 2.87 us
    pallas_call x0 -> x1, Pallas kernels: none -> 151 us  [gather(): pl.pallas_call(functools.partial(gather_kernel, chips), name='gather', ou...]
    unnamed x5 -> x0, waiting for transfers between devices: 119 us -> none
    dot_general x4 -> x2, matrix products: 110 us -> 54.1 us  [the longest x1 28.9 us: step(): lax.dot_general(xg, d_pre, TN, preferred_element_type=F32).astype(BF16)]
    reshape x1 -> x0, waiting for transfers between devices: 26.2 us -> none  [by_group(): a, b = (t.reshape(groups, -1, t.shape[-1]) for t in (a, b))]
    ppermute x0 -> x6, waiting for transfers between devices: none -> 14.8 us  [the longest x1 14.8 us: step(): far0 = lax.ppermute(s_far[:half], 'tp', clockwise)]
    unnamed x3 -> x12, local copies, waits for them, and re-layouts: 13 us -> 1.27 us
    ppermute x0 -> x6, starting transfers between devices: none -> 7.54 us  [the longest x1 3.21 us: step(): far1 = lax.ppermute(s_far[half:], 'tp', counter)]
  transfers between devices with their start and end apart: 3 -> 6, of which waited for: 3 -> 1; matrix products, arithmetic and copies ran while one was open for 43% -> 24% of each run, Pallas kernels for 0% -> 0%
where the time goes in v1:
time: 234 us
  Pallas kernels  151 us (65%)
  matrix products  54.1 us (23%)
  waiting for transfers between devices  14.8 us (6%)
  starting transfers between devices  7.54 us (3%)
  local copies, waits for them, and re-layouts  3.12 us (1%)
  other arithmetic  2.87 us (1%)
    pallas_call x1, Pallas kernels, gather(): pl.pallas_call(functools.partial(gather_kernel, chips), name='gather', ou...  151 us
    dot_general x1, matrix products, step(): lax.dot_general(xg, d_pre, TN, preferred_element_type=F32).astype(BF16)  28.9 us
    dot_general x1, matrix products, step(): lax.dot_general(hidden, dyg, TN, preferred_element_type=F32).astype(BF16)  25.2 us
    ppermute x1, waiting for transfers between devices, step(): far0 = lax.ppermute(s_far[:half], 'tp', clockwise)  14.8 us
  transfers between devices with their start and end apart: 6, of which 1 were waited for; matrix products, arithmetic and copies ran while one was open for 24% of the time, Pallas kernels for 0%

profile of v1, /device:TPU:112, one launch (start us, length us, event | category | flops | bytes accessed | tf_op | source)
XLA Modules:
  0.0 233.8 jit_solution(17751667373259613397)
XLA Ops:
  0.6 150.6 %gather.1 = (bf16[2816,3072]{1,0:T(8,128)(2,1)}, bf16[2816,3072]{1,0:T(8,128)(2,1)}, bf16[2816,1152]{1,0:T(8,128)(2,1)}, f32[352,3072]{1,0:T(8,128)}, bf16[176,3...) custom-call(bf16[352,3072]{1,0:T(8,128)(2,1)} %x.1, ...), custom_call_target="tpu_custom_call" | custom-call | flops 39862665216 | bytes 69206016 | tf_op jit(solution)/shard_map/gather/pallas_call | solution.py:261
  151.3 1.0 collective-permute-start.2
  152.3 1.1 collective-permute-start.3
  153.4 0.0 slice-start.2
  153.4 1.9 fusion.2
  155.2 0.1 collective-permute-start
  155.3 3.2 %collective-permute-start.4 = (bf16[176,3072]{1,0:T(8,128)(2,1)S(1)}, bf16[176,3072]{1,0:T(8,128)(2,1)S(1)}, u32[]{:S(2)}, u32[]{:S(2)}) collective-permute-start(bf16[176,3072]{1,0:T(8,128)(2,1)S(1)} %get-tuple-element.24), channel_id=1, source_target_pairs={{0,6},{1,7},{2,0},{3,1},{4,2},{5,3},{6,4},{7,5},{8,14},{9,15},{10,... | collective-permute-start | bytes 3244040 | tf_op jit(solution)/shard_map/ppermute | solution.py:313
  158.6 0.0 copy-start.1
  158.6 0.0 slice-start.3
  158.6 28.9 %convolution_convert_fusion.1 = bf16[3072,1152]{1,0:T(8,128)(2,1)} fusion(bf16[2816,3072]{1,0:T(8,128)(2,1)} %get-tuple-element.18, bf16[2816,1152]{1,0:T(8,128)(2,1)} %get-tuple-element.19), kind=kOutput, calls=%fused_computation.2 | convolution fusion | flops 19934871552 | bytes 30867456 | tf_op jit(solution)/shard_map/dot_general | solution.py:317
  187.5 14.8 %collective-permute-done = bf16[176,3072]{1,0:T(8,128)(2,1)S(1)} collective-permute-done((bf16[176,3072]{1,0:T(8,128)(2,1)S(1)}, bf16[176,3072]{1,0:T(8,128)(2,1)S(1)}, u32[]{:S(2)}, u32[]{:S(2)}) %collective-permute-start) | collective-permute-done | bytes 1081376 | tf_op jit(solution)/shard_map/ppermute | solution.py:312
  202.3 0.0 copy-done.1
  202.3 0.0 copy-start
  202.3 0.2 add_convert_fusion.3
  202.6 0.1 collective-permute-start.1
  202.7 0.0 collective-permute-done.4
  202.7 1.3 copy-done
  203.9 0.2 add_convert_fusion.1
  204.2 2.0 collective-permute-start.5
  206.2 0.0 slice-start
  206.2 0.0 slice-done.2
  206.2 0.0 slice-done.3
  206.2 0.0 slice-start.1
  206.2 25.2 %convolution_convert_fusion = bf16[1152,3072]{1,0:T(8,128)(2,1)} fusion(bf16[2816,3072]{1,0:T(8,128)(2,1)} %get-tuple-element.20, bf16[2816,1152]{1,0:T(8,128)(2,1)S(1)} %bitcast.6), kind=kOutput, calls=%fused_computation.1 | convolution fusion | flops 19947847680 | bytes 30867456 | tf_op jit(solution)/shard_map/dot_general | solution.py:323
  231.4 0.0 collective-permute-done.2
  231.4 0.0 collective-permute-done.3
  231.4 0.0 collective-permute-done.1
  231.4 0.0 collective-permute-done.5
  231.4 0.0 slice-done
  231.4 0.0 slice-done.1
  231.4 0.9 add_convert_fusion.2
  232.4 1.5 pad_maximum_fusion
  (2 shorter events, 0.0 us)
Async XLA Ops:
  151.3 80.1 %collective-permute-start.2 = (bf16[176,3072]{1,0:T(8,128)(2,1)}, bf16[176,3072]{1,0:T(8,128)(2,1)S(1)}, u32[]{:S(2)}, u32[]{:S(2)}) collective-permute-start(bf16[176,3072]{1,0:T(8,128)(2,1)} %get-tuple-element.15), channel_id=1, source_target_pairs={{0,6},{1,7},{2,0},{3,1},{4,2},{5,3},{6,4},{7,5},{8,14},{9,15},{10,... | collective-permute-start | bytes 3244040 | tf_op jit(solution)/shard_map/ppermute | solution.py:315
  152.3 79.1 %collective-permute-start.3 = (bf16[176,3072]{1,0:T(8,128)(2,1)}, bf16[176,3072]{1,0:T(8,128)(2,1)S(1)}, u32[]{:S(2)}, u32[]{:S(2)}) collective-permute-start(bf16[176,3072]{1,0:T(8,128)(2,1)} %get-tuple-element.16), channel_id=1, source_target_pairs={{0,2},{1,3},{2,4},{3,5},{4,6},{5,7},{6,0},{7,1},{8,10},{9,11},{10,... | collective-permute-start | bytes 3244040 | tf_op jit(solution)/shard_map/ppermute | solution.py:314
  153.4 52.8 %slice-start.2 = ((s8[6488064]{0:T(1024)(128)(4,1)}), s8[4194304]{0:T(1024)(128)(4,1)S(1)}, s32[]{:S(2)}) async-start(s8[6488064]{0:T(1024)(128)(4,1)} %bitcast.5), calls=%async_computation.2 | async-start | bytes 8388608
  155.2 47.1 %collective-permute-start = (bf16[176,3072]{1,0:T(8,128)(2,1)S(1)}, bf16[176,3072]{1,0:T(8,128)(2,1)S(1)}, u32[]{:S(2)}, u32[]{:S(2)}) collective-permute-start(bf16[176,3072]{1,0:T(8,128)(2,1)S(1)} %get-tuple-element.23), channel_id=1, source_target_pairs={{0,2},{1,3},{2,4},{3,5},{4,6},{5,7},{6,0},{7,1},{8,10},{9,11},{10,... | collective-permute-start | bytes 3244040 | tf_op jit(solution)/shard_map/ppermute | solution.py:312
  155.3 47.3 %collective-permute-start.4 = (bf16[176,3072]{1,0:T(8,128)(2,1)S(1)}, bf16[176,3072]{1,0:T(8,128)(2,1)S(1)}, u32[]{:S(2)}, u32[]{:S(2)}) collective-permute-start(bf16[176,3072]{1,0:T(8,128)(2,1)S(1)} %get-tuple-element.24), channel_id=1, source_target_pairs={{0,6},{1,7},{2,0},{3,1},{4,2},{5,3},{6,4},{7,5},{8,14},{9,15},{10,... | collective-permute-start | bytes 3244040 | tf_op jit(solution)/shard_map/ppermute | solution.py:313
  158.6 43.8 %copy-start.1 = (f32[176,3072]{1,0:T(8,128)S(1)}, f32[176,3072]{1,0:T(8,128)}, u32[]{:S(2)}) copy-start(f32[176,3072]{1,0:T(8,128)} %get-tuple-element.13) | copy-start | bytes 6488068
  158.6 47.7 %slice-start.3 = ((s8[6488064]{0:T(1024)(128)(4,1)}), s8[2293760]{0:T(1024)(128)(4,1)S(1)}, s32[]{:S(2)}) async-start(s8[6488064]{0:T(1024)(128)(4,1)} %bitcast.5), calls=%async_computation.3 | async-start | bytes 4587520
  202.3 1.6 copy-start
  202.6 28.8 %collective-permute-start.1 = (bf16[176,3072]{1,0:T(8,128)(2,1)S(1)}, bf16[176,3072]{1,0:T(8,128)(2,1)S(1)}, u32[]{:S(2)}, u32[]{:S(2)}) collective-permute-start(bf16[176,3072]{1,0:T(8,128)(2,1)S(1)} %add_convert_fusion.3), channel_id=1, source_target_pairs={{0,2},{1,3},{2,4},{3,5},{4,6},{5,7},{6,0},{7,1},{8,10},{9,11},{10,... | collective-permute-start | bytes 3244040 | tf_op jit(solution)/shard_map/ppermute | solution.py:319
  204.2 27.2 %collective-permute-start.5 = (bf16[176,3072]{1,0:T(8,128)(2,1)S(1)}, bf16[176,3072]{1,0:T(8,128)(2,1)S(1)}, u32[]{:S(2)}, u32[]{:S(2)}) collective-permute-start(bf16[176,3072]{1,0:T(8,128)(2,1)S(1)} %add_convert_fusion.1), channel_id=1, source_target_pairs={{0,6},{1,7},{2,0},{3,1},{4,2},{5,3},{6,4},{7,5},{8,14},{9,15},{10,... | collective-permute-start | bytes 3244040 | tf_op jit(solution)/shard_map/ppermute | solution.py:320
  206.2 25.2 %slice-start = ((s8[4325376]{0:T(1024)(128)(4,1)}), s8[4194304]{0:T(1024)(128)(4,1)S(1)}, s32[]{:S(2)}) async-start(s8[4325376]{0:T(1024)(128)(4,1)} %bitcast.3), calls=%async_computation | async-start | bytes 8388608
  206.2 25.2 %slice-start.1 = ((s8[4325376]{0:T(1024)(128)(4,1)}), s8[131072]{0:T(1024)(128)(4,1)S(1)}, s32[]{:S(2)}) async-start(s8[4325376]{0:T(1024)(128)(4,1)} %bitcast.3), calls=%async_computation.1 | async-start | bytes 262144

commit v2 on v1

--- a/solution.py
+++ b/solution.py
@@ -18,13 +18,16 @@
 
 def gather_kernel(
     chips, x, dy, pre, w_in, w_down,
-    xg, dyg, d_pre, s_own, s_left0, s_left1, s_right0, s_right1, s_far,
-    wd_v, wi_v, wp_v, dy_v, pre_v, mine_v, other_v, got_v, acc_v, low_v,
-    send_sem, recv_sem, got_send, got_recv, w_send, w_recv, load_sem, store_sem,
+    xg, dyg, d_pre, s_own, go_left, go_right, dw_down,
+    wd_v, wi_v, wp_v, dy_v, pre_v, pair_v, got_v, acc_v, low_v, wait_v, far_v, dw_v,
+    send_sem, recv_sem, got_send, got_recv, w_send, w_recv, far_send, far_recv, load_sem, store_sem,
 ):
     rows, depth = dy.shape
     half = rows // 2
     cols = w_down.shape[0]
+    tile = 384
+    first, top, bottom = pl.ds(0, rows), pl.ds(0, half), pl.ds(half, half)
+    mine_v, other_v = pair_v.at[first], pair_v.at[pl.ds(rows, rows)]
     me = lax.axis_index("tp")
     chip, core = me // CORES, lax.rem(me, CORES)
     left = lax.rem(chip + chips - 1, chips)
@@ -100,7 +103,7 @@
     for target in (to_right, to_left, to_partner):
         pl.semaphore_signal(barrier, inc=1, device_id=target, device_id_type=pl.DeviceIdType.MESH)
     load_wd = pltpu.make_async_copy(w_down, wd_v, load_sem.at[0])
-    load_dy = pltpu.make_async_copy(dy, dy_v, load_sem.at[1])
+    load_dy = pltpu.make_async_copy(dy, dy_v.at[first], load_sem.at[1])
     load_x = pltpu.make_async_copy(x, low_v, load_sem.at[2])
     load_wi = pltpu.make_async_copy(w_in, wi_v, load_sem.at[3])
     load_dy.start()
@@ -117,7 +120,7 @@
     give_w.start()
 
     load_dy.wait()
-    keep_dy = pltpu.make_async_copy(dy_v, block(dyg, chip, core), store_sem.at[0])
+    keep_dy = pltpu.make_async_copy(dy_v.at[first], block(dyg, chip, core), store_sem.at[0])
     keep_dy.start()
     load_x.wait()
     keep_x = pltpu.make_async_copy(low_v, block(xg, chip, core), store_sem.at[1])
@@ -130,19 +133,18 @@
 
     def hidden_grad(stage, k, out_v):
         c = chip_of(stage)
-        load_pre = pltpu.make_async_copy(block(pre, c, k), pre_v, load_sem.at[0])
+        load_pre = pltpu.make_async_copy(block(pre, c, k), pre_v.at[first], load_sem.at[0])
         load_pre.start()
-        load = pltpu.make_async_copy(block(dyg, c, k), dy_v, load_sem.at[1])
+        load = pltpu.make_async_copy(block(dyg, c, k), dy_v.at[first], load_sem.at[1])
         load.start()
         load.wait()
         load_pre.wait()
-        tile = 384
 
         @pl.loop(0, cols // tile)
         def _(t):
             span = pl.ds(pl.multiple_of(t * tile, tile), tile)
-            grad = lax.dot_general(dy_v[...], wd_v[span, :], NT, preferred_element_type=F32)
-            p = pre_v[:, span].astype(F32)
+            grad = lax.dot_general(dy_v[first, :], wd_v[span, :], NT, preferred_element_type=F32)
+            p = pre_v[first, span].astype(F32)
             out_v[:, span] = jnp.where(p > 0, grad * (2.0 * p), 0.0).astype(BF16)
 
         keep = pltpu.make_async_copy(out_v, block(d_pre, c, k), store_sem.at[2])
@@ -157,6 +159,23 @@
 
     keep_dy.wait()
     keep_x.wait()
+    dw_v[...] = jnp.zeros_like(dw_v)
+
+    cut = half // 32 * 16 + 16
+    pieces = [(0, cut, to_right), (cut, half - cut, to_right), (half, cut, to_left), (half + cut, half - cut, to_left)]
+
+    def far_piece(i):
+        start, size, target = pieces[i]
+        span = pl.ds(start, size)
+        return pltpu.make_async_remote_copy(
+            src_ref=low_v.at[span], dst_ref=far_v.at[span], send_sem=far_send.at[i], recv_sem=far_recv.at[i],
+            device_id=target, device_id_type=pl.DeviceIdType.MESH,
+        )
+
+    def put(src, dst, i):
+        copy = pltpu.make_async_copy(src, dst, store_sem.at[i])
+        copy.start()
+        return copy
 
     @pl.loop(0, chips)
     def _(stage):
@@ -198,6 +217,11 @@
         @pl.when(stage == 0)
         def _():
             give_w.wait()
+
+        @pl.when(stage == 3)
+        def _():
+            gx.arrived(R0, L1)
+            gx.start(FR, FL, PL0, PR1)
 
         give.wait_recv()
         wide = 512
@@ -212,33 +236,57 @@
 
         give.wait_send()
         keep.wait()
-        top, bottom = pl.ds(0, half), pl.ds(half, half)
-
-        def put(*pairs):
-            copies = [pltpu.make_async_copy(s, d, store_sem.at[3 + i]) for i, (s, d) in enumerate(pairs)]
-            for copy in copies:
-                copy.start()
-            for copy in copies:
-                copy.wait()
 
         @pl.when(stage == 0)
         def _():
-            put((acc_v, s_own))
+            put(acc_v, s_own, 3).wait()
 
         @pl.when(stage == 1)
         def _():
-            put((low_v.at[top], s_left0), (acc_v.at[bottom], s_left1))
+            wait_v[bottom, :] = acc_v[bottom, :]
+            put(low_v.at[top], go_left.at[top], 3).wait()
 
         @pl.when(stage == 2)
         def _():
-            put((acc_v.at[top], s_right0), (low_v.at[bottom], s_right1))
-
-        @pl.when(stage == 3)
-        def _():
-            put((low_v, s_far))
-
-    gx.arrived(R0, L1)
-    gx.start(FR, FL, PL0, PR1)
+            wait_v[top, :] = acc_v[top, :]
+            put(low_v.at[bottom], go_right.at[bottom], 3).wait()
+
+    for i in (0, 2, 1, 3):
+        far_piece(i).start()
+
+    @pl.loop(0, chips)
+    def _(stage):
+        span = pl.ds(pl.multiple_of(chip_of(stage) * CORES * rows, 16), CORES * rows)
+        load_pre = pltpu.make_async_copy(pre.at[span], pre_v, load_sem.at[0])
+        load = pltpu.make_async_copy(dyg.at[span], dy_v, load_sem.at[1])
+        load_pre.start()
+        load.start()
+        load_pre.wait()
+
+        @pl.loop(0, cols // tile)
+        def _(m):
+            ms = pl.ds(pl.multiple_of(m * tile, tile), tile)
+            pair_v[:, ms] = jnp.square(jnp.maximum(pre_v[:, ms].astype(F32), 0.0)).astype(BF16)
+
+        load.wait()
+
+        @pl.loop(0, cols // tile)
+        def _(m):
+            ms = pl.ds(pl.multiple_of(m * tile, tile), tile)
+
+            @pl.loop(0, CORES)
+            def _(t):
+                wide = depth // CORES
+                ns = pl.ds(pl.multiple_of(t * wide, wide), wide)
+                dw_v[ms, ns] += lax.dot_general(pair_v[:, ms], dy_v[:, ns], TN, preferred_element_type=F32)
+
+    @pl.loop(0, cols // tile)
+    def _(m):
+        ms = pl.ds(pl.multiple_of(m * tile, tile), tile)
+        wd_v[ms, :] = dw_v[ms, :].astype(BF16)
+
+    put_dw = put(wd_v, dw_down, 4)
+
     gx.arrived(R1, L0)
     gx.start(PL1, PR0)
     gx.arrived(FR, FL)
@@ -247,6 +295,17 @@
     gy.sent()
     gx.sent()
 
+    puts = []
+    for i in (0, 2, 1, 3):
+        start, size, _ = pieces[i]
+        span = pl.ds(start, size)
+        far_piece(i).wait()
+        dy_v[span, :] = (wait_v[span, :] + far_v[span, :].astype(F32)).astype(BF16)
+        puts.append(put(dy_v.at[span], (go_right if i < 2 else go_left).at[span], i))
+    for copy in puts:
+        copy.wait()
+    put_dw.wait()
+
 
 def solution(mesh):
     n = mesh.shape["tp"]
@@ -255,7 +314,6 @@
     def gather(x, dy, pre, w_in, w_down):
         rows, depth = x.shape
         tokens, cols = pre.shape
-        half = rows // 2
         anywhere = pl.BlockSpec(memory_space=pl.ANY)
         shape = jax.ShapeDtypeStruct
         return pl.pallas_call(
@@ -266,25 +324,25 @@
                 shape((tokens, depth), BF16),
                 shape((tokens, cols), BF16),
                 shape((rows, depth), F32),
-                shape((half, depth), BF16),
-                shape((half, depth), F32),
-                shape((half, depth), F32),
-                shape((half, depth), BF16),
                 shape((rows, depth), BF16),
+                shape((rows, depth), BF16),
+                shape((cols, depth), BF16),
             ),
             in_specs=[anywhere] * 5,
-            out_specs=(anywhere,) * 9,
+            out_specs=(anywhere,) * 7,
             scratch_shapes=[
                 pltpu.VMEM((cols, depth), BF16),
                 pltpu.VMEM((depth, cols), BF16),
                 pltpu.VMEM((depth, cols), BF16),
-                pltpu.VMEM((rows, depth), BF16),
-                pltpu.VMEM((rows, cols), BF16),
-                pltpu.VMEM((rows, cols), BF16),
-                pltpu.VMEM((rows, cols), BF16),
+                pltpu.VMEM((CORES * rows, depth), BF16),
+                pltpu.VMEM((CORES * rows, cols), BF16),
+                pltpu.VMEM((CORES * rows, cols), BF16),
                 pltpu.VMEM((chips, rows, cols), BF16),
                 pltpu.VMEM((rows, depth), F32),
                 pltpu.VMEM((rows, depth), BF16),
+                pltpu.VMEM((rows, depth), F32),
+                pltpu.VMEM((rows, depth), BF16),
+                pltpu.VMEM((cols, depth), F32),
                 pltpu.SemaphoreType.DMA((2, COPIES)),
                 pltpu.SemaphoreType.DMA((2, COPIES)),
                 pltpu.SemaphoreType.DMA,
@@ -292,39 +350,41 @@
                 pltpu.SemaphoreType.DMA,
                 pltpu.SemaphoreType.DMA,
                 pltpu.SemaphoreType.DMA((4,)),
+                pltpu.SemaphoreType.DMA((4,)),
+                pltpu.SemaphoreType.DMA((4,)),
                 pltpu.SemaphoreType.DMA((5,)),
             ],
             compiler_params=pltpu.CompilerParams(
                 collective_id=0, has_side_effects=True, vmem_limit_bytes=64 * 1024 * 1024 - 65536
             ),
             cost_estimate=pl.CostEstimate(
-                flops=4 * tokens * depth * cols, bytes_accessed=8 * tokens * depth, transcendentals=0
+                flops=6 * tokens * depth * cols, bytes_accessed=8 * tokens * depth, transcendentals=0
             ),
         )(x, dy, pre, w_in, w_down)
 
+    def hand_on(a):
+        rows, depth = a.shape
+        spec = pl.BlockSpec((rows // 8, depth), lambda i: (i, 0))
+
+        def body(a_ref, out_ref):
+            out_ref[...] = a_ref[...]
+
+        return pl.pallas_call(
+            body, name="hand_on", grid=(8,), in_specs=[spec], out_specs=spec, out_shape=jax.ShapeDtypeStruct(a.shape, a.dtype),
+            cost_estimate=pl.CostEstimate(flops=rows * depth * 64, bytes_accessed=4 * rows * depth, transcendentals=0),
+        )(a)
+
     def step(x, dy, pre, w_in, w_down):
-        rows = x.shape[0]
-        half = rows // 2
         clockwise = [(i, (i + CORES) % n) for i in range(n)]
         counter = [(i, (i - CORES) % n) for i in range(n)]
-        xg, dyg, d_pre, s_own, s_left0, s_left1, s_right0, s_right1, s_far = gather(x, dy, pre, w_in, w_down)
-
-        far0 = lax.ppermute(s_far[:half], "tp", clockwise)
-        far1 = lax.ppermute(s_far[half:], "tp", counter)
-        last1 = lax.ppermute(s_right1, "tp", clockwise)
-        last0 = lax.ppermute(s_left0, "tp", counter)
-
+        xg, dyg, d_pre, s_own, go_left, go_right, dw_down = gather(x, dy, pre, w_in, w_down)
+        from_left = lax.ppermute(go_right, "tp", clockwise)
+        from_right = lax.ppermute(go_left, "tp", counter)
         dw_in = lax.dot_general(xg, d_pre, TN, preferred_element_type=F32).astype(BF16)
-
-        sum0 = lax.ppermute((s_right0 + far0.astype(F32)).astype(BF16), "tp", clockwise)
-        sum1 = lax.ppermute((s_left1 + far1.astype(F32)).astype(BF16), "tp", counter)
-
-        hidden = jnp.square(jax.nn.relu(pre.astype(F32))).astype(BF16)
-        dw_down = lax.dot_general(hidden, dyg, TN, preferred_element_type=F32).astype(BF16)
-
-        top = s_own[:half] + sum0.astype(F32) + last0.astype(F32)
-        bottom = s_own[half:] + last1.astype(F32) + sum1.astype(F32)
-        return jnp.concatenate([top, bottom]).astype(BF16), dw_in, dw_down
+        dw_down = hand_on(dw_down)
+        s_own, dw_in, dw_down = lax.optimization_barrier((s_own, dw_in, dw_down))
+        dx = (s_own + from_left.astype(F32) + from_right.astype(F32)).astype(BF16)
+        return dx, dw_in, dw_down
 
     tokens, columns, weight_rows = P(("dp", "tp"), None), P(None, "tp"), P("tp", None)
     return jax.shard_map(

time: 234 us -> 224 us (0.957)
  Pallas kernels: 151 us -> 177 us
  matrix products: 54.1 us -> 28.9 us
  waiting for transfers between devices: 14.8 us -> 9.04 us
  starting transfers between devices: 7.54 us -> 3.31 us
  local copies, waits for them, and re-layouts: 3.12 us -> 0.01 us
    dot_general x1 -> x0, matrix products: 25.2 us -> none  [step(): lax.dot_general(hidden, dyg, TN, preferred_element_type=F32).astype(BF16)]
    pallas_call x1, Pallas kernels: 151 us -> 169 us  [gather(): pl.pallas_call(functools.partial(gather_kernel, chips), name='gather', ou...]
    pallas_call x0 -> x1, Pallas kernels: none -> 8.23 us  [hand_on(): pl.pallas_call(body, name='hand_on', grid=(8,), in_specs=[spec], out_spec...]
    ppermute x6 -> x2, waiting for transfers between devices: 14.8 us -> 9.04 us  [the longest x1 9.04 us: step(): from_left = lax.ppermute(go_right, 'tp', clockwise)]
    ppermute x6 -> x2, starting transfers between devices: 7.54 us -> 3.31 us  [the longest x1 2.14 us: step(): from_right = lax.ppermute(go_left, 'tp', counter)]
    convert_element_type x2 -> x1, other arithmetic: 0.47 us -> 3.88 us  [step(): dx = (s_own + from_left.astype(F32) + from_right.astype(F32)).astype(BF16)]
  transfers between devices with their start and end apart: 6 -> 2, of which waited for: 1 -> 1; matrix products, arithmetic and copies ran while one was open for 24% -> 13% of each run, Pallas kernels for 0% -> 4%
where the time goes in v2:
time: 224 us; the launch traced here: 223 us
  Pallas kernels  177 us (79%)
  matrix products  28.9 us (13%)
  waiting for transfers between devices  9.04 us (4%)
  other arithmetic  3.88 us (2%)
  starting transfers between devices  3.31 us (1%)
    pallas_call x1, Pallas kernels, gather(): pl.pallas_call(functools.partial(gather_kernel, chips), name='gather', ou...  169 us
    dot_general x1, matrix products, step(): lax.dot_general(xg, d_pre, TN, preferred_element_type=F32).astype(BF16)  28.9 us
    ppermute x1, waiting for transfers between devices, step(): from_left = lax.ppermute(go_right, 'tp', clockwise)  9.04 us
    pallas_call x1, Pallas kernels, hand_on(): pl.pallas_call(body, name='hand_on', grid=(8,), in_specs=[spec], out_spec...  8.23 us
  transfers between devices with their start and end apart: 2, of which 1 were waited for; matrix products, arithmetic and copies ran while one was open for 13% of the time, Pallas kernels for 4%

profile of v2, /device:TPU:112, one launch (start us, length us, event | category | flops | bytes accessed | tf_op | source)
XLA Modules:
  0.0 223.3 jit_solution(10122141010852561446)
XLA Ops:
  0.6 169.3 %gather.1 = (bf16[2816,3072]{1,0:T(8,128)(2,1)}, bf16[2816,3072]{1,0:T(8,128)(2,1)}, bf16[2816,1152]{1,0:T(8,128)(2,1)}, f32[352,3072]{1,0:T(8,128)}, bf16[352,3...) custom-call(bf16[352,3072]{1,0:T(8,128)(2,1)} %x.1, bf16[352,3072]{1,0:T(8,128)(2,1)} %dy.1, ...), custom_call_target="tpu_custom_call" | custom-call | flops 59793997824 | bytes 69206016 | tf_op jit(solution)/shard_map/gather/pallas_call | solution.py:319
  169.9 1.2 collective-permute-start
  171.1 2.1 collective-permute-start.1
  173.2 0.0 slice-start
  173.2 8.2 %hand_on.1 = bf16[1152,3072]{1,0:T(8,128)(2,1)} custom-call(bf16[1152,3072]{1,0:T(8,128)(2,1)} %get-tuple-element.15.a_ref), custom_call_target="tpu_custom_call" | custom-call | flops 226492416 | bytes 14155776 | tf_op jit(solution)/shard_map/hand_on/pallas_call | solution.py:372
  181.4 0.0 slice-start.1
  181.4 28.9 %convolution_convert_fusion = bf16[3072,1152]{1,0:T(8,128)(2,1)} fusion(bf16[2816,3072]{1,0:T(8,128)(2,1)} %get-tuple-element.13, bf16[2816,1152]{1,0:T(8,128)(2,1)} %get-tuple-element.14), kind=kOutput, calls=%fused_computation | convolution fusion | flops 19934871552 | bytes 30867456 | tf_op jit(solution)/shard_map/dot_general | solution.py:383
  210.4 9.0 %collective-permute-done = bf16[352,3072]{1,0:T(8,128)(2,1)S(1)} collective-permute-done((bf16[352,3072]{1,0:T(8,128)(2,1)}, bf16[352,3072]{1,0:T(8,128)(2,1)S(1)}, u32[]{:S(2)}, u32[]{:S(2)}) %collective-permute-start) | collective-permute-done | bytes 2162720 | tf_op jit(solution)/shard_map/ppermute | solution.py:381
  219.4 0.0 collective-permute-done.1
  219.4 0.0 slice-done
  219.4 0.0 slice-done.1
  219.4 3.9 %add_convert_fusion = bf16[352,3072]{1,0:T(8,128)(2,1)} fusion(bf16[352,3072]{1,0:T(8,128)(2,1)} %collective-permute-done.1, f32[352,3072]{1,0:T(8,128)S(1)} %bitcast.3, bf16[352,3072]{1,0:T(8,128)(2,1)S(1)} %collective-permute-done), kind=kLoop, calls=%fused_computation.1 | loop fusion | flops 5406720 | bytes 10813440 | tf_op jit(solution)/shard_map/convert_element_type | solution.py:386
  (1 shorter events, 0.0 us)
Async XLA Ops:
  169.9 49.5 %collective-permute-start = (bf16[352,3072]{1,0:T(8,128)(2,1)}, bf16[352,3072]{1,0:T(8,128)(2,1)S(1)}, u32[]{:S(2)}, u32[]{:S(2)}) collective-permute-start(bf16[352,3072]{1,0:T(8,128)(2,1)} %get-tuple-element.17), channel_id=1, source_target_pairs={{0,2},{1,3},{2,4},{3,5},{4,6},{5,7},{6,0},{7,1},{8,10},{9,11},{10,... | collective-permute-start | bytes 6488072 | tf_op jit(solution)/shard_map/ppermute | solution.py:381
  171.1 48.3 %collective-permute-start.1 = (bf16[352,3072]{1,0:T(8,128)(2,1)}, bf16[352,3072]{1,0:T(8,128)(2,1)}, u32[]{:S(2)}, u32[]{:S(2)}) collective-permute-start(bf16[352,3072]{1,0:T(8,128)(2,1)} %get-tuple-element.18), channel_id=1, source_target_pairs={{0,6},{1,7},{2,0},{3,1},{4,2},{5,3},{6,4},{7,5},{8,14},{9,15},{10,... | collective-permute-start | bytes 6488072 | tf_op jit(solution)/shard_map/ppermute | solution.py:382
  173.2 46.2 %slice-start = ((s8[4325376]{0:T(1024)(128)(4,1)}), s8[131072]{0:T(1024)(128)(4,1)S(1)}, s32[]{:S(2)}) async-start(s8[4325376]{0:T(1024)(128)(4,1)} %bitcast.2), calls=%async_computation | async-start | bytes 262144
  181.4 38.0 %slice-start.1 = ((s8[4325376]{0:T(1024)(128)(4,1)}), s8[4194304]{0:T(1024)(128)(4,1)S(1)}, s32[]{:S(2)}) async-start(s8[4325376]{0:T(1024)(128)(4,1)} %bitcast.2), calls=%async_computation.1 | async-start | bytes 8388608

commit v3 on v2

--- a/solution.py
+++ b/solution.py
@@ -8,6 +8,7 @@
 from jax.sharding import PartitionSpec as P
 
 CORES = 2
+LATE = 64
 F32, BF16 = jnp.float32, jnp.bfloat16
 NT = (((1,), (1,)), ((), ()))
 TN = (((0,), (0,)), ((), ()))
@@ -18,7 +19,7 @@
 
 def gather_kernel(
     chips, x, dy, pre, w_in, w_down,
-    xg, dyg, d_pre, s_own, go_left, go_right, dw_down,
+    xg, dyg, d_pre, s_own, go_left, go_left_late, go_right, go_right_late, dw_down,
     wd_v, wi_v, wp_v, dy_v, pre_v, pair_v, got_v, acc_v, low_v, wait_v, far_v, dw_v,
     send_sem, recv_sem, got_send, got_recv, w_send, w_recv, far_send, far_recv, load_sem, store_sem,
 ):
@@ -111,6 +112,7 @@
     pl.semaphore_wait(barrier, 3)
 
     gy.start(R0, L1, OWN, R1, L0)
+    gx.start(R0, L1)
     load_x.start()
     load_wi.start()
     give_w = pltpu.make_async_remote_copy(
@@ -161,7 +163,7 @@
     keep_x.wait()
     dw_v[...] = jnp.zeros_like(dw_v)
 
-    cut = half // 32 * 16 + 16
+    cut = half - (rows - go_left.shape[0])
     pieces = [(0, cut, to_right), (cut, half - cut, to_right), (half, cut, to_left), (half + cut, half - cut, to_left)]
 
     def far_piece(i):
@@ -183,12 +185,14 @@
         def _():
             gy.arrived(R0, L1)
             gy.start(FR, FL, PL0, PR1)
-            gx.start(R0, L1, R1, L0, OWN)
+            gx.start(R1, L0, OWN)
             gy.arrived(R1, L0)
             gy.start(PL1, PR0)
 
         @pl.when(stage == 3)
         def _():
+            gx.arrived(R0, L1)
+            gx.start(FR, FL, PL0, PR1)
             gy.arrived(FR, FL)
             gy.start(PO0, PO1)
 
@@ -217,11 +221,6 @@
         @pl.when(stage == 0)
         def _():
             give_w.wait()
-
-        @pl.when(stage == 3)
-        def _():
-            gx.arrived(R0, L1)
-            gx.start(FR, FL, PL0, PR1)
 
         give.wait_recv()
         wide = 512
@@ -249,7 +248,11 @@
         @pl.when(stage == 2)
         def _():
             wait_v[top, :] = acc_v[top, :]
-            put(low_v.at[bottom], go_right.at[bottom], 3).wait()
+            early = go_right.shape[0]
+            a = put(low_v.at[pl.ds(half, early - half)], go_right.at[pl.ds(half, early - half)], 3)
+            b = put(low_v.at[pl.ds(early, rows - early)], go_right_late, 2)
+            a.wait()
+            b.wait()
 
     for i in (0, 2, 1, 3):
         far_piece(i).start()
@@ -301,7 +304,8 @@
         span = pl.ds(start, size)
         far_piece(i).wait()
         dy_v[span, :] = (wait_v[span, :] + far_v[span, :].astype(F32)).astype(BF16)
-        puts.append(put(dy_v.at[span], (go_right if i < 2 else go_left).at[span], i))
+        target = go_left_late if i == 3 else (go_right if i < 2 else go_left).at[span]
+        puts.append(put(dy_v.at[span], target, i))
     for copy in puts:
         copy.wait()
     put_dw.wait()
@@ -314,6 +318,7 @@
     def gather(x, dy, pre, w_in, w_down):
         rows, depth = x.shape
         tokens, cols = pre.shape
+        early = rows - LATE
         anywhere = pl.BlockSpec(memory_space=pl.ANY)
         shape = jax.ShapeDtypeStruct
         return pl.pallas_call(
@@ -324,12 +329,14 @@
                 shape((tokens, depth), BF16),
                 shape((tokens, cols), BF16),
                 shape((rows, depth), F32),
-                shape((rows, depth), BF16),
-                shape((rows, depth), BF16),
+                shape((early, depth), BF16),
+                shape((rows - early, depth), BF16),
+                shape((early, depth), BF16),
+                shape((rows - early, depth), BF16),
                 shape((cols, depth), BF16),
             ),
             in_specs=[anywhere] * 5,
-            out_specs=(anywhere,) * 7,
+            out_specs=(anywhere,) * 9,
             scratch_shapes=[
                 pltpu.VMEM((cols, depth), BF16),
                 pltpu.VMEM((depth, cols), BF16),
@@ -374,16 +381,35 @@
             cost_estimate=pl.CostEstimate(flops=rows * depth * 64, bytes_accessed=4 * rows * depth, transcendentals=0),
         )(a)
 
+    def add_kernel(own, one, other, *refs):
+        refs[-1][...] = (own[...] + one[...].astype(F32) + other[...].astype(F32)).astype(BF16)
+
+    def final_sum(own, one, other, start, block, so_far=None):
+        rows, depth = own.shape
+        moved = pl.BlockSpec((block, depth), lambda i: (start // block + i, 0))
+        plain = pl.BlockSpec((block, depth), lambda i: (i, 0))
+        before = [] if so_far is None else [so_far]
+        return pl.pallas_call(
+            add_kernel, name="final_sum", grid=(one.shape[0] // block,),
+            in_specs=[moved, plain, plain] + [pl.BlockSpec(memory_space=pl.ANY) for _ in before],
+            out_specs=moved, out_shape=jax.ShapeDtypeStruct((rows, depth), BF16),
+            input_output_aliases={3: 0} if before else {},
+            cost_estimate=pl.CostEstimate(flops=one.size * 64, bytes_accessed=10 * one.size, transcendentals=0),
+        )(own, one, other, *before)
+
     def step(x, dy, pre, w_in, w_down):
         clockwise = [(i, (i + CORES) % n) for i in range(n)]
         counter = [(i, (i - CORES) % n) for i in range(n)]
-        xg, dyg, d_pre, s_own, go_left, go_right, dw_down = gather(x, dy, pre, w_in, w_down)
+        xg, dyg, d_pre, s_own, go_left, go_left_late, go_right, go_right_late, dw_down = gather(x, dy, pre, w_in, w_down)
         from_left = lax.ppermute(go_right, "tp", clockwise)
         from_right = lax.ppermute(go_left, "tp", counter)
+        from_left_late = lax.ppermute(go_right_late, "tp", clockwise)
+        from_right_late = lax.ppermute(go_left_late, "tp", counter)
         dw_in = lax.dot_general(xg, d_pre, TN, preferred_element_type=F32).astype(BF16)
         dw_down = hand_on(dw_down)
         s_own, dw_in, dw_down = lax.optimization_barrier((s_own, dw_in, dw_down))
-        dx = (s_own + from_left.astype(F32) + from_right.astype(F32)).astype(BF16)
+        dx = final_sum(s_own, from_left, from_right, 0, 96)
+        dx = final_sum(s_own, from_left_late, from_right_late, from_left.shape[0], 32, dx)
         return dx, dw_in, dw_down
 
     tokens, columns, weight_rows = P(("dp", "tp"), None), P(None, "tp"), P("tp", None)

time: 224 us -> 230 us (1.027)
  Pallas kernels: 177 us -> 184 us
  other arithmetic: 3.88 us -> 0 us
  starting transfers between devices: 3.31 us -> 6.55 us
  waiting for transfers between devices: 9.04 us -> 6 us
  local copies, waits for them, and re-layouts: 0.01 us -> 2.43 us
    pallas_call x0 -> x2, Pallas kernels: none -> 7.09 us  [final_sum(): pl.pallas_call(add_kernel, name='final_sum', grid=(one.shape[0] // block,...]
    convert_element_type x1 -> x0, other arithmetic: 3.88 us -> none  [step(): dx = (s_own + from_left.astype(F32) + from_right.astype(F32)).astype(BF16)]
    ppermute x0 -> x2, starting transfers between devices: none -> 3.31 us  [the longest x1 2.14 us: step(): from_right_late = lax.ppermute(go_left_late, 'tp', counter)]
    ppermute x1, waiting for transfers between devices: 9.04 us -> 5.99 us  [step(): from_left = lax.ppermute(go_right, 'tp', clockwise)]
    unnamed x4, local copies, waits for them, and re-layouts: 0.01 us -> 2.43 us
  transfers between devices with their start and end apart: 2 -> 4, of which waited for: 1 -> 1; matrix products, arithmetic and copies ran while one was open for 13% -> 13% of each run, Pallas kernels for 4% -> 6%
where the time goes in v3:
time: 230 us; the launch traced here: 229 us
  Pallas kernels  184 us (80%)
  matrix products  28.8 us (13%)
  starting transfers between devices  6.55 us (3%)
  waiting for transfers between devices  6 us (3%)
  local copies, waits for them, and re-layouts  2.43 us (1%)
    pallas_call x1, Pallas kernels, gather(): pl.pallas_call(functools.partial(gather_kernel, chips), name='gather', ou...  169 us
    dot_general x1, matrix products, step(): lax.dot_general(xg, d_pre, TN, preferred_element_type=F32).astype(BF16)  28.8 us
    pallas_call x1, Pallas kernels, hand_on(): pl.pallas_call(body, name='hand_on', grid=(8,), in_specs=[spec], out_spec...  8.19 us
    pallas_call x2, Pallas kernels, final_sum(): pl.pallas_call(add_kernel, name='final_sum', grid=(one.shape[0] // block,...  7.09 us
    ppermute x1, waiting for transfers between devices, step(): from_left = lax.ppermute(go_right, 'tp', clockwise)  5.99 us
  transfers between devices with their start and end apart: 4, of which 1 were waited for; matrix products, arithmetic and copies ran while one was open for 13% of the time, Pallas kernels for 6%

profile of v3, /device:TPU:112, one launch (start us, length us, event | category | flops | bytes accessed | tf_op | source)
XLA Modules:
  0.0 228.8 jit_solution(3973558768737190960)
XLA Ops:
  0.6 169.2 %gather.1 = (bf16[2816,3072]{1,0:T(8,128)(2,1)}, bf16[2816,3072]{1,0:T(8,128)(2,1)}, bf16[2816,1152]{1,0:T(8,128)(2,1)}, f32[352,3072]{1,0:T(8,128)}, bf16[288,3...) custom-call(bf16[352,3072]{1,0:T(8,128)(2,1)} %x.1, ...), custom_call_target="tpu_custom_call" | custom-call | flops 59793997824 | bytes 69206016 | tf_op jit(solution)/shard_map/gather/pallas_call | solution.py:324
  169.8 1.2 collective-permute-start
  171.0 2.1 collective-permute-start.1
  173.1 0.0 collective-permute-start.2
  173.1 3.2 %collective-permute-start.3 = (bf16[288,3072]{1,0:T(8,128)(2,1)}, bf16[288,3072]{1,0:T(8,128)(2,1)S(1)}, u32[]{:S(2)}, u32[]{:S(2)}) collective-permute-start(bf16[288,3072]{1,0:T(8,128)(2,1)} %get-tuple-element.22), channel_id=1, source_target_pairs={{0,6},{1,7},{2,0},{3,1},{4,2},{5,3},{6,4},{7,5},{8,14},{9,15},{10,... | collective-permute-start | bytes 5308424 | tf_op jit(solution)/shard_map/ppermute | solution.py:405
  176.4 28.8 %convolution_convert_fusion = bf16[3072,1152]{1,0:T(8,128)(2,1)} fusion(bf16[2816,3072]{1,0:T(8,128)(2,1)} %get-tuple-element.15, bf16[2816,1152]{1,0:T(8,128)(2,1)} %get-tuple-element.16), kind=kOutput, calls=%fused_computation | convolution fusion | flops 19934871552 | bytes 30867456 | tf_op jit(solution)/shard_map/dot_general | solution.py:408
  205.1 8.2 %hand_on.1 = bf16[1152,3072]{1,0:T(8,128)(2,1)} custom-call(bf16[1152,3072]{1,0:T(8,128)(2,1)} %get-tuple-element.17.a_ref), custom_call_target="tpu_custom_call" | custom-call | flops 226492416 | bytes 14155776 | tf_op jit(solution)/shard_map/hand_on/pallas_call | solution.py:379
  213.3 6.0 %collective-permute-done.2.one = bf16[288,3072]{1,0:T(8,128)(2,1)S(1)} collective-permute-done((bf16[288,3072]{1,0:T(8,128)(2,1)}, bf16[288,3072]{1,0:T(8,128)(2,1)S(1)}, u32[]{:S(2)}, u32[]{:S(2)}) %collective-permute-start.2) | collective-permute-done | bytes 1769504 | tf_op jit(solution)/shard_map/ppermute | solution.py:404
  219.3 0.0 copy-start
  219.3 0.0 collective-permute-done.3.other
  219.3 1.2 copy-done
  220.6 0.0 copy-start.1
  220.6 1.2 copy-done.1
  221.7 4.9 %final_sum.2.refs_0_ = bf16[352,3072]{1,0:T(8,128)(2,1)} custom-call(f32[352,3072]{1,0:T(8,128)} %get-tuple-element.18.own, bf16[288,3072]{1,0:T(8,128)(2,1)} %copy-done, bf16[288,3072]{1,0:T(8,128)(2,1)} %copy-done.1), custom_call_target="tpu_custom_call" | custom-call | flops 56623104 | bytes 8847360 | tf_op jit(solution)/shard_map/final_sum/pallas_call | solution.py:392
  226.7 0.0 collective-permute-done.one
  226.7 0.0 collective-permute-done.1.other
  226.7 2.2 final_sum.3
Async XLA Ops:
  169.8 56.9 %collective-permute-start = (bf16[64,3072]{1,0:T(8,128)(2,1)}, bf16[64,3072]{1,0:T(8,128)(2,1)}, u32[]{:S(2)}, u32[]{:S(2)}) collective-permute-start(bf16[64,3072]{1,0:T(8,128)(2,1)} %get-tuple-element.19), channel_id=1, source_target_pairs={{0,2},{1,3},{2,4},{3,5},{4,6},{5,7},{6,0},{7,1},{8,10},{9,11},{10,... | collective-permute-start | bytes 1179656 | tf_op jit(solution)/shard_map/ppermute | solution.py:406
  171.0 55.7 %collective-permute-start.1 = (bf16[64,3072]{1,0:T(8,128)(2,1)}, bf16[64,3072]{1,0:T(8,128)(2,1)}, u32[]{:S(2)}, u32[]{:S(2)}) collective-permute-start(bf16[64,3072]{1,0:T(8,128)(2,1)} %get-tuple-element.20), channel_id=1, source_target_pairs={{0,6},{1,7},{2,0},{3,1},{4,2},{5,3},{6,4},{7,5},{8,14},{9,15},{10,... | collective-permute-start | bytes 1179656 | tf_op jit(solution)/shard_map/ppermute | solution.py:407
  173.1 46.2 %collective-permute-start.2 = (bf16[288,3072]{1,0:T(8,128)(2,1)}, bf16[288,3072]{1,0:T(8,128)(2,1)S(1)}, u32[]{:S(2)}, u32[]{:S(2)}) collective-permute-start(bf16[288,3072]{1,0:T(8,128)(2,1)} %get-tuple-element.21), channel_id=1, source_target_pairs={{0,2},{1,3},{2,4},{3,5},{4,6},{5,7},{6,0},{7,1},{8,10},{9,11},{10,... | collective-permute-start | bytes 5308424 | tf_op jit(solution)/shard_map/ppermute | solution.py:404
  173.1 46.2 %collective-permute-start.3 = (bf16[288,3072]{1,0:T(8,128)(2,1)}, bf16[288,3072]{1,0:T(8,128)(2,1)S(1)}, u32[]{:S(2)}, u32[]{:S(2)}) collective-permute-start(bf16[288,3072]{1,0:T(8,128)(2,1)} %get-tuple-element.22), channel_id=1, source_target_pairs={{0,6},{1,7},{2,0},{3,1},{4,2},{5,3},{6,4},{7,5},{8,14},{9,15},{10,... | collective-permute-start | bytes 5308424 | tf_op jit(solution)/shard_map/ppermute | solution.py:405
  219.3 1.2 copy-start
  220.6 1.2 copy-start.1

commit v4 on v2

--- a/solution.py
+++ b/solution.py
@@ -7,7 +7,9 @@
 from jax.experimental.pallas import tpu as pltpu
 from jax.sharding import PartitionSpec as P
 
+
 CORES = 2
+LATE, EDGE = 64, 32
 F32, BF16 = jnp.float32, jnp.bfloat16
 NT = (((1,), (1,)), ((), ()))
 TN = (((0,), (0,)), ((), ()))
@@ -18,9 +20,9 @@
 
 def gather_kernel(
     chips, x, dy, pre, w_in, w_down,
-    xg, dyg, d_pre, s_own, go_left, go_right, dw_down,
-    wd_v, wi_v, wp_v, dy_v, pre_v, pair_v, got_v, acc_v, low_v, wait_v, far_v, dw_v,
-    send_sem, recv_sem, got_send, got_recv, w_send, w_recv, far_send, far_recv, load_sem, store_sem,
+    xg, dyg, d_pre, s_own, s_own_late, go_left, go_left_late, go_right, go_right_late, got_left, got_right, dw_down,
+    wd_v, wi_v, wp_v, dy_v, pre_v, pair_v, got_v, acc_v, low_v, wait_v, far_v, hold_v, dw_v,
+    send_sem, recv_sem, got_send, got_recv, w_send, w_recv, far_send, far_recv, hold_send, hold_recv, load_sem, store_sem,
 ):
     rows, depth = dy.shape
     half = rows // 2
@@ -111,6 +113,7 @@
     pl.semaphore_wait(barrier, 3)
 
     gy.start(R0, L1, OWN, R1, L0)
+    gx.start(R0, L1)
     load_x.start()
     load_wi.start()
     give_w = pltpu.make_async_remote_copy(
@@ -161,17 +164,33 @@
     keep_x.wait()
     dw_v[...] = jnp.zeros_like(dw_v)
 
-    cut = half // 32 * 16 + 16
-    pieces = [(0, cut, to_right), (cut, half - cut, to_right), (half, cut, to_left), (half + cut, half - cut, to_left)]
+    edge, late = got_left.shape[0], go_left_late.shape[0]
+    mid, end = rows - edge - late, rows - edge
+    cut = half // 32 * 16
+    pieces = [
+        (0, cut, to_right, go_right.at[pl.ds(0, cut)]),
+        (cut, half - cut, to_right, go_right.at[pl.ds(cut, half - cut)]),
+        (half, mid - half, to_left, go_left.at[pl.ds(half - edge, mid - half)]),
+        (mid, late, to_left, go_left_late),
+        (end, edge, to_left, go_left.at[pl.ds(mid - edge, edge)]),
+    ]
+    order = (0, 2, 1, 3, 4)
 
     def far_piece(i):
-        start, size, target = pieces[i]
+        start, size, target, _ = pieces[i]
         span = pl.ds(start, size)
         return pltpu.make_async_remote_copy(
             src_ref=low_v.at[span], dst_ref=far_v.at[span], send_sem=far_send.at[i], recv_sem=far_recv.at[i],
             device_id=target, device_id_type=pl.DeviceIdType.MESH,
         )
 
+    def held_piece(i):
+        return pltpu.make_async_remote_copy(
+            src_ref=hold_v.at[pl.ds(i * edge, edge)], dst_ref=(got_right, got_left)[i],
+            send_sem=hold_send.at[i], recv_sem=hold_recv.at[i],
+            device_id=(to_left, to_right)[i], device_id_type=pl.DeviceIdType.MESH,
+        )
+
     def put(src, dst, i):
         copy = pltpu.make_async_copy(src, dst, store_sem.at[i])
         copy.start()
@@ -183,12 +202,14 @@
         def _():
             gy.arrived(R0, L1)
             gy.start(FR, FL, PL0, PR1)
-            gx.start(R0, L1, R1, L0, OWN)
+            gx.start(R1, L0, OWN)
             gy.arrived(R1, L0)
             gy.start(PL1, PR0)
 
         @pl.when(stage == 3)
         def _():
+            gx.arrived(R0, L1)
+            gx.start(FR, FL, PL0, PR1)
             gy.arrived(FR, FL)
             gy.start(PO0, PO1)
 
@@ -217,11 +238,6 @@
         @pl.when(stage == 0)
         def _():
             give_w.wait()
-
-        @pl.when(stage == 3)
-        def _():
-            gx.arrived(R0, L1)
-            gx.start(FR, FL, PL0, PR1)
 
         give.wait_recv()
         wide = 512
@@ -239,20 +255,35 @@
 
         @pl.when(stage == 0)
         def _():
-            put(acc_v, s_own, 3).wait()
+            puts = [
+                put(acc_v.at[pl.ds(0, mid)], s_own.at[pl.ds(0, mid)], 1),
+                put(acc_v.at[pl.ds(mid, late)], s_own_late, 2),
+                put(acc_v.at[pl.ds(end, edge)], s_own.at[pl.ds(mid, edge)], 3),
+            ]
+            for copy in puts:
+                copy.wait()
 
         @pl.when(stage == 1)
         def _():
             wait_v[bottom, :] = acc_v[bottom, :]
-            put(low_v.at[top], go_left.at[top], 3).wait()
+            hold_v[pl.ds(0, edge), :] = low_v[pl.ds(0, edge), :]
+            put(low_v.at[pl.ds(edge, half - edge)], go_left.at[pl.ds(0, half - edge)], 3).wait()
 
         @pl.when(stage == 2)
         def _():
             wait_v[top, :] = acc_v[top, :]
-            put(low_v.at[bottom], go_right.at[bottom], 3).wait()
-
-    for i in (0, 2, 1, 3):
+            hold_v[pl.ds(edge, edge), :] = low_v[pl.ds(end, edge), :]
+            puts = [
+                put(low_v.at[pl.ds(half, mid - half)], go_right.at[pl.ds(half, mid - half)], 2),
+                put(low_v.at[pl.ds(mid, late)], go_right_late, 3),
+            ]
+            for copy in puts:
+                copy.wait()
+
+    for i in order:
         far_piece(i).start()
+    for i in range(2):
+        held_piece(i).start()
 
     @pl.loop(0, chips)
     def _(stage):
@@ -296,15 +327,17 @@
     gx.sent()
 
     puts = []
-    for i in (0, 2, 1, 3):
-        start, size, _ = pieces[i]
+    for i in order:
+        start, size, _, target = pieces[i]
         span = pl.ds(start, size)
         far_piece(i).wait()
         dy_v[span, :] = (wait_v[span, :] + far_v[span, :].astype(F32)).astype(BF16)
-        puts.append(put(dy_v.at[span], (go_right if i < 2 else go_left).at[span], i))
+        puts.append(put(dy_v.at[span], target, (0, 1, 2, 3, 5)[i]))
     for copy in puts:
         copy.wait()
     put_dw.wait()
+    for i in range(2):
+        held_piece(i).wait()
 
 
 def solution(mesh):
@@ -314,6 +347,7 @@
     def gather(x, dy, pre, w_in, w_down):
         rows, depth = x.shape
         tokens, cols = pre.shape
+        early = rows - EDGE - LATE
         anywhere = pl.BlockSpec(memory_space=pl.ANY)
         shape = jax.ShapeDtypeStruct
         return pl.pallas_call(
@@ -323,13 +357,18 @@
                 shape((tokens, depth), BF16),
                 shape((tokens, depth), BF16),
                 shape((tokens, cols), BF16),
-                shape((rows, depth), F32),
-                shape((rows, depth), BF16),
-                shape((rows, depth), BF16),
+                shape((rows - LATE, depth), F32),
+                shape((LATE, depth), F32),
+                shape((early, depth), BF16),
+                shape((LATE, depth), BF16),
+                shape((early, depth), BF16),
+                shape((LATE, depth), BF16),
+                shape((EDGE, depth), BF16),
+                shape((EDGE, depth), BF16),
                 shape((cols, depth), BF16),
             ),
             in_specs=[anywhere] * 5,
-            out_specs=(anywhere,) * 7,
+            out_specs=(anywhere,) * 12,
             scratch_shapes=[
                 pltpu.VMEM((cols, depth), BF16),
                 pltpu.VMEM((depth, cols), BF16),
@@ -342,6 +381,7 @@
                 pltpu.VMEM((rows, depth), BF16),
                 pltpu.VMEM((rows, depth), F32),
                 pltpu.VMEM((rows, depth), BF16),
+                pltpu.VMEM((2 * EDGE, depth), BF16),
                 pltpu.VMEM((cols, depth), F32),
                 pltpu.SemaphoreType.DMA((2, COPIES)),
                 pltpu.SemaphoreType.DMA((2, COPIES)),
@@ -349,10 +389,12 @@
                 pltpu.SemaphoreType.DMA((chips,)),
                 pltpu.SemaphoreType.DMA,
                 pltpu.SemaphoreType.DMA,
+                pltpu.SemaphoreType.DMA((5,)),
+                pltpu.SemaphoreType.DMA((5,)),
+                pltpu.SemaphoreType.DMA((2,)),
+                pltpu.SemaphoreType.DMA((2,)),
                 pltpu.SemaphoreType.DMA((4,)),
-                pltpu.SemaphoreType.DMA((4,)),
-                pltpu.SemaphoreType.DMA((4,)),
-                pltpu.SemaphoreType.DMA((5,)),
+                pltpu.SemaphoreType.DMA((6,)),
             ],
             compiler_params=pltpu.CompilerParams(
                 collective_id=0, has_side_effects=True, vmem_limit_bytes=64 * 1024 * 1024 - 65536
@@ -362,28 +404,50 @@
             ),
         )(x, dy, pre, w_in, w_down)
 
-    def hand_on(a):
-        rows, depth = a.shape
-        spec = pl.BlockSpec((rows // 8, depth), lambda i: (i, 0))
-
-        def body(a_ref, out_ref):
-            out_ref[...] = a_ref[...]
-
+    def weight_grad(xg, d_pre, done, tile=384):
+        tokens, depth = xg.shape
+        cols = d_pre.shape[1]
+        steps = depth // tile
+
+        def body(x_ref, d_ref, done_ref, out_ref, copy_ref):
+            copy_ref[...] = done_ref[...]
+            out_ref[...] = lax.dot_general(x_ref[...], d_ref[...], TN, preferred_element_type=F32).astype(BF16)
+
+        side = pl.BlockSpec((done.shape[0] // steps, done.shape[1]), lambda i: (i, 0))
         return pl.pallas_call(
-            body, name="hand_on", grid=(8,), in_specs=[spec], out_specs=spec, out_shape=jax.ShapeDtypeStruct(a.shape, a.dtype),
-            cost_estimate=pl.CostEstimate(flops=rows * depth * 64, bytes_accessed=4 * rows * depth, transcendentals=0),
-        )(a)
+            body, name="weight_grad", grid=(steps,),
+            in_specs=[pl.BlockSpec((tokens, tile), lambda i: (0, i)), pl.BlockSpec((tokens, cols), lambda i: (0, 0)), side],
+            out_specs=(pl.BlockSpec((tile, cols), lambda i: (i, 0)), side),
+            out_shape=(jax.ShapeDtypeStruct((depth, cols), BF16), jax.ShapeDtypeStruct(done.shape, done.dtype)),
+            compiler_params=pltpu.CompilerParams(vmem_limit_bytes=62 * 1024 * 1024),
+            cost_estimate=pl.CostEstimate(
+                flops=2 * tokens * depth * cols, bytes_accessed=2 * tokens * (depth + cols) + 6 * depth * cols, transcendentals=0
+            ),
+        )(xg, d_pre, done)
 
     def step(x, dy, pre, w_in, w_down):
         clockwise = [(i, (i + CORES) % n) for i in range(n)]
         counter = [(i, (i - CORES) % n) for i in range(n)]
-        xg, dyg, d_pre, s_own, go_left, go_right, dw_down = gather(x, dy, pre, w_in, w_down)
+        (
+            xg, _, d_pre, s_own, s_own_late, go_left, go_left_late, go_right, go_right_late, got_left, got_right, dw_down
+        ) = gather(x, dy, pre, w_in, w_down)
         from_left = lax.ppermute(go_right, "tp", clockwise)
         from_right = lax.ppermute(go_left, "tp", counter)
-        dw_in = lax.dot_general(xg, d_pre, TN, preferred_element_type=F32).astype(BF16)
-        dw_down = hand_on(dw_down)
+        from_left_late = lax.ppermute(go_right_late, "tp", clockwise)
+        from_right_late = lax.ppermute(go_left_late, "tp", counter)
+        dw_in, dw_down = weight_grad(xg, d_pre, dw_down)
         s_own, dw_in, dw_down = lax.optimization_barrier((s_own, dw_in, dw_down))
-        dx = (s_own + from_left.astype(F32) + from_right.astype(F32)).astype(BF16)
+        mid = go_right.shape[0]
+        one, other, top, bottom = (t.astype(F32) for t in (from_left, from_right, got_right, got_left))
+        dx = jnp.concatenate([
+            s_own[:EDGE] + one[:EDGE] + top,
+            s_own[EDGE:mid] + one[EDGE:] + other[:mid - EDGE],
+            jnp.zeros_like(s_own_late),
+            s_own[mid:] + bottom + other[mid - EDGE:],
+        ]).astype(BF16)
+        dx = lax.optimization_barrier(dx)
+        late = s_own_late + from_left_late.astype(F32) + from_right_late.astype(F32)
+        dx = lax.dynamic_update_slice(dx, late.astype(BF16), (mid, 0))
         return dx, dw_in, dw_down
 
     tokens, columns, weight_rows = P(("dp", "tp"), None), P(None, "tp"), P("tp", None)

time: 224 us -> 222 us (level)
  matrix products: 28.9 us -> 0 us
  Pallas kernels: 177 us -> 202 us
  waiting for transfers between devices: 9.04 us -> 4.26 us
  starting transfers between devices: 3.31 us -> 6.55 us
  local copies, waits for them, and re-layouts: 0.01 us -> 3.23 us
    dot_general x1 -> x0, matrix products: 28.9 us -> none  [step(): lax.dot_general(xg, d_pre, TN, preferred_element_type=F32).astype(BF16)]
    pallas_call x1, Pallas kernels: 8.23 us -> 29.2 us  [weight_grad(): pl.pallas_call(body, name='weight_grad', grid=(steps,), in_specs=[pl.Bloc...]
    ppermute x1, waiting for transfers between devices: 9.04 us -> 3.1 us  [step(): from_left = lax.ppermute(go_right, 'tp', clockwise)]
    pallas_call x1, Pallas kernels: 169 us -> 173 us  [gather(): pl.pallas_call(functools.partial(gather_kernel, chips), name='gather', ou...]
    ppermute x0 -> x2, starting transfers between devices: none -> 3.24 us  [the longest x1 3.23 us: step(): from_right_late = lax.ppermute(go_left_late, 'tp', counter)]
    unnamed x4 -> x10, local copies, waits for them, and re-layouts: 0.01 us -> 3.22 us
  transfers between devices with their start and end apart: 2 -> 4, of which waited for: 1 -> 2; matrix products, arithmetic and copies ran while one was open for 13% -> 2% of each run, Pallas kernels for 4% -> 13%
where the time goes in v4:
time: 222 us; the launch traced here: 221 us
  Pallas kernels  202 us (91%)
  starting transfers between devices  6.55 us (3%)
  other arithmetic  4.66 us (2%)
  waiting for transfers between devices  4.26 us (2%)
  local copies, waits for them, and re-layouts  3.23 us (1%)
    pallas_call x1, Pallas kernels, gather(): pl.pallas_call(functools.partial(gather_kernel, chips), name='gather', ou...  173 us
    pallas_call x1, Pallas kernels, weight_grad(): pl.pallas_call(body, name='weight_grad', grid=(steps,), in_specs=[pl.Bloc...  29.2 us
  transfers between devices with their start and end apart: 4, of which 2 were waited for; matrix products, arithmetic and copies ran while one was open for 2% of the time, Pallas kernels for 13%

profile of v4, /device:TPU:112, one launch (start us, length us, event | category | flops | bytes accessed | tf_op | source)
XLA Modules:
  0.0 221.4 jit_solution(2523251049617912153)
XLA Ops:
  0.6 172.8 %gather.1 = (bf16[2816,3072]{1,0:T(8,128)(2,1)}, bf16[2816,3072]{1,0:T(8,128)(2,1)}, bf16[2816,1152]{1,0:T(8,128)(2,1)}, f32[288,3072]{1,0:T(8,128)}, f32[64,307...) custom-call(bf16[352,3072]{1,0:T(8,128)(2,1)} %x.1, ...), custom_call_target="tpu_custom_call" | custom-call | flops 59793997824 | bytes 69206016 | tf_op jit(solution)/shard_map/gather/pallas_call | solution.py:353
  173.4 1.2 collective-permute-start
  174.6 2.1 collective-permute-start.1
  176.8 0.0 collective-permute-start.2
  176.8 3.2 %collective-permute-start.3 = (bf16[64,3072]{1,0:T(8,128)(2,1)}, bf16[64,3072]{1,0:T(8,128)(2,1)}, u32[]{:S(2)}, u32[]{:S(2)}) collective-permute-start(bf16[64,3072]{1,0:T(8,128)(2,1)} %get-tuple-element.32), channel_id=1, source_target_pairs={{0,6},{1,7},{2,0},{3,1},{4,2},{5,3},{6,4},{7,5},{8,14},{9,15},{10,... | collective-permute-start | bytes 1179656 | tf_op jit(solution)/shard_map/ppermute | solution.py:437
  180.0 29.2 %weight_grad.1 = (bf16[3072,1152]{1,0:T(8,128)(2,1)}, bf16[1152,3072]{1,0:T(8,128)(2,1)}) custom-call(bf16[2816,3072]{1,0:T(8,128)(2,1)} %get-tuple-element.20.x_ref, bf16[2816,1152]{1,0:T(8,128)(2,1)} %get-tuple-element.21.d_ref, bf16[1152,3072]{1,0:T(8,128)(2,1)} %get-tuple-element.22.done_ref), custom_call_target="tpu_custom_call" | custom-call | flops 19931332608 | bytes 45023232 | tf_op jit(solution)/shard_map/weight_grad/pallas_call | solution.py:417
  209.2 3.1 %collective-permute-done = bf16[256,3072]{1,0:T(8,128)(2,1)} collective-permute-done((bf16[256,3072]{1,0:T(8,128)(2,1)}, bf16[256,3072]{1,0:T(8,128)(2,1)}, u32[]{:S(2)}, u32[]{:S(2)}) %collective-permute-start) | collective-permute-done | bytes 1572896 | tf_op jit(solution)/shard_map/ppermute | solution.py:434
  212.3 1.8 convert_element_type.22
  214.1 0.0 copy-start
  214.1 0.0 collective-permute-done.1
  214.1 0.4 convert_element_type.24
  214.5 1.6 copy-done
  216.1 0.0 copy-start.3
  216.1 0.0 copy-start.4
  216.1 0.8 fusion
  216.9 0.2 copy-done.3
  217.0 0.1 copy-done.4
  217.1 0.0 copy-start.2
  217.1 0.1 fusion.4
  217.2 0.6 pad_maximum_fusion
  217.8 1.2 collective-permute-done.2
  219.0 0.0 collective-permute-done.3
  219.0 0.0 copy-done.2
  219.0 1.1 fusion.1
  220.1 0.0 copy-start.1
  220.1 1.3 copy-done.1
  (2 shorter events, 0.0 us)
Async XLA Ops:
  173.4 38.9 %collective-permute-start = (bf16[256,3072]{1,0:T(8,128)(2,1)}, bf16[256,3072]{1,0:T(8,128)(2,1)}, u32[]{:S(2)}, u32[]{:S(2)}) collective-permute-start(bf16[256,3072]{1,0:T(8,128)(2,1)} %get-tuple-element.26), channel_id=1, source_target_pairs={{0,2},{1,3},{2,4},{3,5},{4,6},{5,7},{6,0},{7,1},{8,10},{9,11},{10,... | collective-permute-start | bytes 4718600 | tf_op jit(solution)/shard_map/ppermute | solution.py:434
  174.6 39.5 %collective-permute-start.1 = (bf16[256,3072]{1,0:T(8,128)(2,1)}, bf16[256,3072]{1,0:T(8,128)(2,1)S(1)}, u32[]{:S(2)}, u32[]{:S(2)}) collective-permute-start(bf16[256,3072]{1,0:T(8,128)(2,1)} %get-tuple-element.28), channel_id=1, source_target_pairs={{0,6},{1,7},{2,0},{3,1},{4,2},{5,3},{6,4},{7,5},{8,14},{9,15},{10,... | collective-permute-start | bytes 4718600 | tf_op jit(solution)/shard_map/ppermute | solution.py:435
  176.8 42.2 %collective-permute-start.2 = (bf16[64,3072]{1,0:T(8,128)(2,1)}, bf16[64,3072]{1,0:T(8,128)(2,1)S(1)}, u32[]{:S(2)}, u32[]{:S(2)}) collective-permute-start(bf16[64,3072]{1,0:T(8,128)(2,1)} %get-tuple-element.31), channel_id=1, source_target_pairs={{0,2},{1,3},{2,4},{3,5},{4,6},{5,7},{6,0},{7,1},{8,10},{9,11},{10,... | collective-permute-start | bytes 1179656 | tf_op jit(solution)/shard_map/ppermute | solution.py:436
  176.8 42.2 %collective-permute-start.3 = (bf16[64,3072]{1,0:T(8,128)(2,1)}, bf16[64,3072]{1,0:T(8,128)(2,1)}, u32[]{:S(2)}, u32[]{:S(2)}) collective-permute-start(bf16[64,3072]{1,0:T(8,128)(2,1)} %get-tuple-element.32), channel_id=1, source_target_pairs={{0,6},{1,7},{2,0},{3,1},{4,2},{5,3},{6,4},{7,5},{8,14},{9,15},{10,... | collective-permute-start | bytes 1179656 | tf_op jit(solution)/shard_map/ppermute | solution.py:437
  214.1 2.0 copy-start
  216.1 0.9 copy-start.3
  216.1 1.0 copy-start.4
  217.1 1.8 copy-start.2
  220.1 1.3 copy-start.1

commit v5 on v4

--- a/solution.py
+++ b/solution.py
@@ -425,6 +425,13 @@
             ),
         )(xg, d_pre, done)
 
+    def keep_in_hbm(a):
+        anywhere = pl.BlockSpec(memory_space=pl.ANY)
+        return pl.pallas_call(
+            lambda a_ref, out_ref: None, name="keep_in_hbm", in_specs=[anywhere], out_specs=anywhere,
+            out_shape=jax.ShapeDtypeStruct(a.shape, a.dtype), input_output_aliases={0: 0},
+        )(a)
+
     def step(x, dy, pre, w_in, w_down):
         clockwise = [(i, (i + CORES) % n) for i in range(n)]
         counter = [(i, (i - CORES) % n) for i in range(n)]
@@ -445,7 +452,7 @@
             jnp.zeros_like(s_own_late),
             s_own[mid:] + bottom + other[mid - EDGE:],
         ]).astype(BF16)
-        dx = lax.optimization_barrier(dx)
+        dx = keep_in_hbm(dx)
         late = s_own_late + from_left_late.astype(F32) + from_right_late.astype(F32)
         dx = lax.dynamic_update_slice(dx, late.astype(BF16), (mid, 0))
         return dx, dw_in, dw_down

time: 222 us -> 223 us (level)
  transfers between devices with their start and end apart: 4 -> 4, of which waited for: 2 -> 1; matrix products, arithmetic and copies ran while one was open for 2% -> 2% of each run, Pallas kernels for 13% -> 13%
where the time goes in v5:
time: 223 us; the launch traced here: 222 us
  Pallas kernels  202 us (91%)
  other arithmetic  6.75 us (3%)
  starting transfers between devices  6.55 us (3%)
  waiting for transfers between devices  3.11 us (1%)
  local copies, waits for them, and re-layouts  3.01 us (1%)
    pallas_call x1, Pallas kernels, gather(): pl.pallas_call(functools.partial(gather_kernel, chips), name='gather', ou...  173 us
    pallas_call x1, Pallas kernels, weight_grad(): pl.pallas_call(body, name='weight_grad', grid=(steps,), in_specs=[pl.Bloc...  29.2 us
  transfers between devices with their start and end apart: 4, of which 1 were waited for; matrix products, arithmetic and copies ran while one was open for 2% of the time, Pallas kernels for 13%

profile of v5, /device:TPU:112, one launch (start us, length us, event | category | flops | bytes accessed | tf_op | source)
XLA Modules:
  0.0 222.1 jit_solution(8503260344359904782)
XLA Ops:
  0.6 172.8 %gather.1 = (bf16[2816,3072]{1,0:T(8,128)(2,1)}, bf16[2816,3072]{1,0:T(8,128)(2,1)}, bf16[2816,1152]{1,0:T(8,128)(2,1)}, f32[288,3072]{1,0:T(8,128)}, f32[64,307...) custom-call(bf16[352,3072]{1,0:T(8,128)(2,1)} %x.1, ...), custom_call_target="tpu_custom_call" | custom-call | flops 59793997824 | bytes 69206016 | tf_op jit(solution)/shard_map/gather/pallas_call | solution.py:353
  173.4 1.2 collective-permute-start
  174.6 2.1 collective-permute-start.1
  176.8 0.0 collective-permute-start.2
  176.8 3.2 %collective-permute-start.3 = (bf16[64,3072]{1,0:T(8,128)(2,1)}, bf16[64,3072]{1,0:T(8,128)(2,1)}, u32[]{:S(2)}, u32[]{:S(2)}) collective-permute-start(bf16[64,3072]{1,0:T(8,128)(2,1)} %get-tuple-element.32), channel_id=1, source_target_pairs={{0,6},{1,7},{2,0},{3,1},{4,2},{5,3},{6,4},{7,5},{8,14},{9,15},{10,... | collective-permute-start | bytes 1179656 | tf_op jit(solution)/shard_map/ppermute | solution.py:444
  180.0 29.2 %weight_grad.1 = (bf16[3072,1152]{1,0:T(8,128)(2,1)}, bf16[1152,3072]{1,0:T(8,128)(2,1)}) custom-call(bf16[2816,3072]{1,0:T(8,128)(2,1)} %get-tuple-element.20.x_ref, bf16[2816,1152]{1,0:T(8,128)(2,1)} %get-tuple-element.21.d_ref, bf16[1152,3072]{1,0:T(8,128)(2,1)} %get-tuple-element.22.done_ref), custom_call_target="tpu_custom_call" | custom-call | flops 19931332608 | bytes 45023232 | tf_op jit(solution)/shard_map/weight_grad/pallas_call | solution.py:417
  209.2 3.1 %collective-permute-done = bf16[256,3072]{1,0:T(8,128)(2,1)} collective-permute-done((bf16[256,3072]{1,0:T(8,128)(2,1)}, bf16[256,3072]{1,0:T(8,128)(2,1)}, u32[]{:S(2)}, u32[]{:S(2)}) %collective-permute-start) | collective-permute-done | bytes 1572896 | tf_op jit(solution)/shard_map/ppermute | solution.py:441
  212.3 1.8 convert_element_type.22
  214.1 0.0 copy-start
  214.1 0.0 collective-permute-done.1
  214.1 0.4 convert_element_type.24
  214.5 1.6 copy-done
  216.1 0.0 copy-start.2
  216.1 0.0 copy-start.3
  216.1 0.8 fusion
  216.9 0.2 copy-done.2
  217.0 0.1 copy-done.3
  217.1 0.1 fusion.4
  217.2 1.9 pad_maximum_fusion.a_ref
  219.1 0.0 copy-start.1
  219.1 0.0 collective-permute-done.2
  219.1 0.0 collective-permute-done.3
  219.2 1.1 copy-done.1
  220.3 1.9 fusion.1
  (3 shorter events, 0.0 us)
Async XLA Ops:
  173.4 38.9 %collective-permute-start = (bf16[256,3072]{1,0:T(8,128)(2,1)}, bf16[256,3072]{1,0:T(8,128)(2,1)}, u32[]{:S(2)}, u32[]{:S(2)}) collective-permute-start(bf16[256,3072]{1,0:T(8,128)(2,1)} %get-tuple-element.26), channel_id=1, source_target_pairs={{0,2},{1,3},{2,4},{3,5},{4,6},{5,7},{6,0},{7,1},{8,10},{9,11},{10,... | collective-permute-start | bytes 4718600 | tf_op jit(solution)/shard_map/ppermute | solution.py:441
  174.6 39.5 %collective-permute-start.1 = (bf16[256,3072]{1,0:T(8,128)(2,1)}, bf16[256,3072]{1,0:T(8,128)(2,1)S(1)}, u32[]{:S(2)}, u32[]{:S(2)}) collective-permute-start(bf16[256,3072]{1,0:T(8,128)(2,1)} %get-tuple-element.28), channel_id=1, source_target_pairs={{0,6},{1,7},{2,0},{3,1},{4,2},{5,3},{6,4},{7,5},{8,14},{9,15},{10,... | collective-permute-start | bytes 4718600 | tf_op jit(solution)/shard_map/ppermute | solution.py:442
  176.8 42.4 %collective-permute-start.2 = (bf16[64,3072]{1,0:T(8,128)(2,1)}, bf16[64,3072]{1,0:T(8,128)(2,1)S(1)}, u32[]{:S(2)}, u32[]{:S(2)}) collective-permute-start(bf16[64,3072]{1,0:T(8,128)(2,1)} %get-tuple-element.31), channel_id=1, source_target_pairs={{0,2},{1,3},{2,4},{3,5},{4,6},{5,7},{6,0},{7,1},{8,10},{9,11},{10,... | collective-permute-start | bytes 1179656 | tf_op jit(solution)/shard_map/ppermute | solution.py:443
  176.8 42.4 %collective-permute-start.3 = (bf16[64,3072]{1,0:T(8,128)(2,1)}, bf16[64,3072]{1,0:T(8,128)(2,1)}, u32[]{:S(2)}, u32[]{:S(2)}) collective-permute-start(bf16[64,3072]{1,0:T(8,128)(2,1)} %get-tuple-element.32), channel_id=1, source_target_pairs={{0,6},{1,7},{2,0},{3,1},{4,2},{5,3},{6,4},{7,5},{8,14},{9,15},{10,... | collective-permute-start | bytes 1179656 | tf_op jit(solution)/shard_map/ppermute | solution.py:444
  214.1 2.0 copy-start
  216.1 0.9 copy-start.2
  216.1 1.0 copy-start.3
  219.1 1.1 copy-start.1

commit v6 on v5

--- a/solution.py
+++ b/solution.py
@@ -9,7 +9,7 @@
 
 
 CORES = 2
-LATE, EDGE = 64, 32
+LATE, EDGE = 32, 32
 F32, BF16 = jnp.float32, jnp.bfloat16
 NT = (((1,), (1,)), ((), ()))
 TN = (((0,), (0,)), ((), ()))
@@ -20,7 +20,7 @@
 
 def gather_kernel(
     chips, x, dy, pre, w_in, w_down,
-    xg, dyg, d_pre, s_own, s_own_late, go_left, go_left_late, go_right, go_right_late, got_left, got_right, dw_down,
+    xg, dyg, d_pre, s_own, go_left, go_left_late, go_right, go_right_late, got_left, got_right, dw_down,
     wd_v, wi_v, wp_v, dy_v, pre_v, pair_v, got_v, acc_v, low_v, wait_v, far_v, hold_v, dw_v,
     send_sem, recv_sem, got_send, got_recv, w_send, w_recv, far_send, far_recv, hold_send, hold_recv, load_sem, store_sem,
 ):
@@ -255,13 +255,7 @@
 
         @pl.when(stage == 0)
         def _():
-            puts = [
-                put(acc_v.at[pl.ds(0, mid)], s_own.at[pl.ds(0, mid)], 1),
-                put(acc_v.at[pl.ds(mid, late)], s_own_late, 2),
-                put(acc_v.at[pl.ds(end, edge)], s_own.at[pl.ds(mid, edge)], 3),
-            ]
-            for copy in puts:
-                copy.wait()
+            put(acc_v, s_own, 3).wait()
 
         @pl.when(stage == 1)
         def _():
@@ -357,8 +351,7 @@
                 shape((tokens, depth), BF16),
                 shape((tokens, depth), BF16),
                 shape((tokens, cols), BF16),
-                shape((rows - LATE, depth), F32),
-                shape((LATE, depth), F32),
+                shape((rows, depth), F32),
                 shape((early, depth), BF16),
                 shape((LATE, depth), BF16),
                 shape((early, depth), BF16),
@@ -368,7 +361,7 @@
                 shape((cols, depth), BF16),
             ),
             in_specs=[anywhere] * 5,
-            out_specs=(anywhere,) * 12,
+            out_specs=(anywhere,) * 11,
             scratch_shapes=[
                 pltpu.VMEM((cols, depth), BF16),
                 pltpu.VMEM((depth, cols), BF16),
@@ -419,7 +412,7 @@
             in_specs=[pl.BlockSpec((tokens, tile), lambda i: (0, i)), pl.BlockSpec((tokens, cols), lambda i: (0, 0)), side],
             out_specs=(pl.BlockSpec((tile, cols), lambda i: (i, 0)), side),
             out_shape=(jax.ShapeDtypeStruct((depth, cols), BF16), jax.ShapeDtypeStruct(done.shape, done.dtype)),
-            compiler_params=pltpu.CompilerParams(vmem_limit_bytes=62 * 1024 * 1024),
+            compiler_params=pltpu.CompilerParams(vmem_limit_bytes=55 * 1024 * 1024),
             cost_estimate=pl.CostEstimate(
                 flops=2 * tokens * depth * cols, bytes_accessed=2 * tokens * (depth + cols) + 6 * depth * cols, transcendentals=0
             ),
@@ -436,7 +429,7 @@
         clockwise = [(i, (i + CORES) % n) for i in range(n)]
         counter = [(i, (i - CORES) % n) for i in range(n)]
         (
-            xg, _, d_pre, s_own, s_own_late, go_left, go_left_late, go_right, go_right_late, got_left, got_right, dw_down
+            xg, _, d_pre, s_own, go_left, go_left_late, go_right, go_right_late, got_left, got_right, dw_down
         ) = gather(x, dy, pre, w_in, w_down)
         from_left = lax.ppermute(go_right, "tp", clockwise)
         from_right = lax.ppermute(go_left, "tp", counter)
@@ -445,15 +438,15 @@
         dw_in, dw_down = weight_grad(xg, d_pre, dw_down)
         s_own, dw_in, dw_down = lax.optimization_barrier((s_own, dw_in, dw_down))
         mid = go_right.shape[0]
-        one, other, top, bottom = (t.astype(F32) for t in (from_left, from_right, got_right, got_left))
+        lower, upper = from_left[EDGE:], from_right[:mid - EDGE]
         dx = jnp.concatenate([
-            s_own[:EDGE] + one[:EDGE] + top,
-            s_own[EDGE:mid] + one[EDGE:] + other[:mid - EDGE],
-            jnp.zeros_like(s_own_late),
-            s_own[mid:] + bottom + other[mid - EDGE:],
+            s_own[:EDGE] + from_left[:EDGE].astype(F32) + got_right.astype(F32),
+            s_own[EDGE:mid] + lower.astype(F32) + upper.astype(F32),
+            jnp.zeros_like(s_own[:LATE]),
+            s_own[mid + LATE:] + got_left.astype(F32) + from_right[mid - EDGE:].astype(F32),
         ]).astype(BF16)
         dx = keep_in_hbm(dx)
-        late = s_own_late + from_left_late.astype(F32) + from_right_late.astype(F32)
+        late = s_own[mid:mid + LATE] + from_left_late.astype(F32) + from_right_late.astype(F32)
         dx = lax.dynamic_update_slice(dx, late.astype(BF16), (mid, 0))
         return dx, dw_in, dw_down
 

time: 223 us -> 221 us (level)
  waiting for transfers between devices: 3.11 us -> 7.01 us
  local copies, waits for them, and re-layouts: 3.01 us -> 0.09 us
  other arithmetic: 6.75 us -> 4.46 us
    ppermute x1, waiting for transfers between devices: 3.1 us -> 7 us  [step(): from_left = lax.ppermute(go_right, 'tp', clockwise)]
    unnamed x8 -> x6, local copies, waits for them, and re-layouts: 3 us -> 0.01 us
  transfers between devices with their start and end apart: 4 -> 4, of which waited for: 1 -> 1; matrix products, arithmetic and copies ran while one was open for 2% -> 1% of each run, Pallas kernels for 13% -> 13%
where the time goes in v6:
time: 221 us
  Pallas kernels  202 us (91%)
  waiting for transfers between devices  7.01 us (3%)
  starting transfers between devices  6.55 us (3%)
  other arithmetic  4.46 us (2%)
    pallas_call x1, Pallas kernels, gather(): pl.pallas_call(functools.partial(gather_kernel, chips), name='gather', ou...  173 us
    pallas_call x1, Pallas kernels, weight_grad(): pl.pallas_call(body, name='weight_grad', grid=(steps,), in_specs=[pl.Bloc...  29.3 us
    ppermute x1, waiting for transfers between devices, step(): from_left = lax.ppermute(go_right, 'tp', clockwise)  7 us
  transfers between devices with their start and end apart: 4, of which 1 were waited for; matrix products, arithmetic and copies ran while one was open for 1% of the time, Pallas kernels for 13%

profile of v6, /device:TPU:112, one launch (start us, length us, event | category | flops | bytes accessed | tf_op | source)
XLA Modules:
  0.0 220.9 jit_solution(15344028999175312174)
XLA Ops:
  0.6 172.8 %gather.1 = (bf16[2816,3072]{1,0:T(8,128)(2,1)}, bf16[2816,3072]{1,0:T(8,128)(2,1)}, bf16[2816,1152]{1,0:T(8,128)(2,1)}, f32[352,3072]{1,0:T(8,128)}, bf16[288,3...) custom-call(bf16[352,3072]{1,0:T(8,128)(2,1)} %x.1, ...), custom_call_target="tpu_custom_call" | custom-call | flops 59793997824 | bytes 69206016 | tf_op jit(solution)/shard_map/gather/pallas_call | solution.py:347
  173.4 1.2 collective-permute-start
  174.6 2.1 collective-permute-start.1
  176.8 0.0 collective-permute-start.2
  176.8 3.2 %collective-permute-start.3 = (bf16[32,3072]{1,0:T(8,128)(2,1)}, bf16[32,3072]{1,0:T(8,128)(2,1)S(1)}, u32[]{:S(2)}, u32[]{:S(2)}) collective-permute-start(bf16[32,3072]{1,0:T(8,128)(2,1)} %get-tuple-element.30), channel_id=1, source_target_pairs={{0,6},{1,7},{2,0},{3,1},{4,2},{5,3},{6,4},{7,5},{8,14},{9,15},{10,... | collective-permute-start | bytes 589832 | tf_op jit(solution)/shard_map/ppermute | solution.py:437
  180.0 0.0 copy-start
  180.0 29.3 %weight_grad.1 = (bf16[3072,1152]{1,0:T(8,128)(2,1)}, bf16[1152,3072]{1,0:T(8,128)(2,1)}) custom-call(bf16[2816,3072]{1,0:T(8,128)(2,1)} %get-tuple-element.19.x_ref, bf16[2816,1152]{1,0:T(8,128)(2,1)} %get-tuple-element.20.d_ref, bf16[1152,3072]{1,0:T(8,128)(2,1)} %get-tuple-element.21.done_ref), custom_call_target="tpu_custom_call" | custom-call | flops 19931332608 | bytes 45023232 | tf_op jit(solution)/shard_map/weight_grad/pallas_call | solution.py:410
  209.3 0.1 pad.2.clone
  209.4 0.0 copy-start.1
  209.4 0.0 copy-start.2
  209.4 7.0 %collective-permute-done = bf16[288,3072]{1,0:T(8,128)(2,1)S(1)} collective-permute-done((bf16[288,3072]{1,0:T(8,128)(2,1)}, bf16[288,3072]{1,0:T(8,128)(2,1)S(1)}, u32[]{:S(2)}, u32[]{:S(2)}) %collective-permute-start) | collective-permute-done | bytes 1769504 | tf_op jit(solution)/shard_map/ppermute | solution.py:434
  216.4 0.0 collective-permute-done.1
  216.4 0.0 copy-done
  216.4 0.7 add_convert_fusion
  217.1 0.0 copy-done.1
  217.1 0.0 copy-done.2
  217.1 0.1 add_convert_fusion.3
  217.3 1.9 pad_maximum_fusion.a_ref
  219.2 0.0 collective-permute-done.2
  219.2 0.0 collective-permute-done.3
  219.2 1.7 fusion
  (2 shorter events, 0.0 us)
Async XLA Ops:
  173.4 43.0 %collective-permute-start = (bf16[288,3072]{1,0:T(8,128)(2,1)}, bf16[288,3072]{1,0:T(8,128)(2,1)S(1)}, u32[]{:S(2)}, u32[]{:S(2)}) collective-permute-start(bf16[288,3072]{1,0:T(8,128)(2,1)} %get-tuple-element.25), channel_id=1, source_target_pairs={{0,2},{1,3},{2,4},{3,5},{4,6},{5,7},{6,0},{7,1},{8,10},{9,11},{10,... | collective-permute-start | bytes 5308424 | tf_op jit(solution)/shard_map/ppermute | solution.py:434
  174.6 41.8 %collective-permute-start.1 = (bf16[288,3072]{1,0:T(8,128)(2,1)}, bf16[288,3072]{1,0:T(8,128)(2,1)S(1)}, u32[]{:S(2)}, u32[]{:S(2)}) collective-permute-start(bf16[288,3072]{1,0:T(8,128)(2,1)} %get-tuple-element.27), channel_id=1, source_target_pairs={{0,6},{1,7},{2,0},{3,1},{4,2},{5,3},{6,4},{7,5},{8,14},{9,15},{10,... | collective-permute-start | bytes 5308424 | tf_op jit(solution)/shard_map/ppermute | solution.py:435
  176.8 42.4 %collective-permute-start.2 = (bf16[32,3072]{1,0:T(8,128)(2,1)}, bf16[32,3072]{1,0:T(8,128)(2,1)S(1)}, u32[]{:S(2)}, u32[]{:S(2)}) collective-permute-start(bf16[32,3072]{1,0:T(8,128)(2,1)} %get-tuple-element.29), channel_id=1, source_target_pairs={{0,2},{1,3},{2,4},{3,5},{4,6},{5,7},{6,0},{7,1},{8,10},{9,11},{10,... | collective-permute-start | bytes 589832 | tf_op jit(solution)/shard_map/ppermute | solution.py:436
  176.8 42.4 %collective-permute-start.3 = (bf16[32,3072]{1,0:T(8,128)(2,1)}, bf16[32,3072]{1,0:T(8,128)(2,1)S(1)}, u32[]{:S(2)}, u32[]{:S(2)}) collective-permute-start(bf16[32,3072]{1,0:T(8,128)(2,1)} %get-tuple-element.30), channel_id=1, source_target_pairs={{0,6},{1,7},{2,0},{3,1},{4,2},{5,3},{6,4},{7,5},{8,14},{9,15},{10,... | collective-permute-start | bytes 589832 | tf_op jit(solution)/shard_map/ppermute | solution.py:437
  180.0 36.4 %copy-start = (f32[352,3072]{1,0:T(8,128)S(1)}, f32[352,3072]{1,0:T(8,128)}, u32[]{:S(2)}) copy-start(f32[352,3072]{1,0:T(8,128)} %get-tuple-element.24) | copy-start | bytes 12976132
  209.4 7.7 %copy-start.1 = (bf16[32,3072]{1,0:T(8,128)(2,1)S(1)}, bf16[32,3072]{1,0:T(8,128)(2,1)}, u32[]{:S(2)}) copy-start(bf16[32,3072]{1,0:T(8,128)(2,1)} %get-tuple-element.28) | copy-start | bytes 589828
  209.4 7.7 %copy-start.2 = (bf16[32,3072]{1,0:T(8,128)(2,1)S(1)}, bf16[32,3072]{1,0:T(8,128)(2,1)}, u32[]{:S(2)}) copy-start(bf16[32,3072]{1,0:T(8,128)(2,1)} %get-tuple-element.26) | copy-start | bytes 589828
